TPU v7x, 256 devices: a whole 4x4x8 slice. The times are simulated.
256 devices in a mesh: gx: 32 (over y, z), gz: 8 (over x, core).
Axes of the slice: x: 4, y: 4, z: 8, core: 2. Of those that a mesh axis runs over, the one named last changes fastest.
Arguments:
- flow_state: float32 [4, 512, 256, 128], P(None, 'gx', 'gz'), may hold values from -6 to 6
- slot_ids: int32 [2048], P(('gx', 'gz')), may hold values from -1 to 1023, as said below
- corners: int32 [3, 2048], P(None, ('gx', 'gz')), may hold values from 0 to 511, as said below
- marker_cells: int32 [3, 2048, 512], P(None, ('gx', 'gz')), may hold values from 1 to 21
- marker_frac: float32 [3, 2048, 512], P(None, ('gx', 'gz')), may hold values from 0 to 1
- particle_velocity: float32 [3, 1024], replicated, may hold values from -4 to 4
- particle_spin: float32 [3, 1024], replicated, may hold values from -0.6 to 0.6
Outputs:
- velocity: float32 [3, 512, 256, 128], P(None, 'gx', 'gz')
- source: float32 [2, 128, 256, 512], P(None, 'gz', 'gx')
Inputs may be any that keep to these rules, and one draw needn't show every extreme that they name: `slot_ids`: the ids of the particles that a tile's device owns stand in its 8 slots and -1 in each empty slot; every id 0 to 1023 stands in exactly one slot; some device has all of its slots full. corners[:, s] is the first cell of the box of slot s; the box's x and z ranges wrap around the grid; the cells (corners[0, s] + 12) mod 512 and (corners[2, s] + 12) mod 256 lie in the x and z ranges of the tile whose device holds slot s, and corners[1, s] <= 104.
All inputs are finite; a program needn't handle non-finite values.
Results may differ from a plain program's by a relative error of at most 0.0003.
Values sent between devices are 32-bit elements; how exact they have to be, the bound alone decides.
A program may use at most 64 MiB of HBM per device.

v0:
```python
import functools
import math

import jax
import jax.numpy as jnp
import numpy as np
from jax import lax
from jax.experimental import pallas as pl
from jax.experimental.pallas import tpu as pltpu
from jax.sharding import PartitionSpec as P

BOX = 24
HALF = 12
BAND = 32
STEP = 8
SIDE = 16
MESH = pl.DeviceIdType.MESH


time_step = 0.1
viscosity = 0.2
drive_force = 1.0


def padded_2(array, sides):
    for axis, dim, width in sides:
        devices, length = (lax.axis_size(axis), array.shape[dim])
        up = [(i, (i + 1) % devices) for i in range(devices)]
        down = [(j, i) for i, j in up]
        last = lax.slice_in_dim(array, length - width, length, axis=dim)
        first = lax.slice_in_dim(array, 0, width, axis=dim)
        before = lax.ppermute(last, axis, up)
        after = lax.ppermute(first, axis, down)
        array = jnp.concatenate([before, array, after], axis=dim)
    return array


def with_halo(array, sides, width):
    edges = {}
    for axis, dim in sides:
        devices, length = (lax.axis_size(axis), array.shape[dim])
        up = [(i, (i + 1) % devices) for i in range(devices)]
        last = lax.slice_in_dim(array, length - width, length, axis=dim)
        first = lax.slice_in_dim(array, 0, width, axis=dim)
        edges[dim] = (
            lax.ppermute(last, axis, up),
            lax.ppermute(first, axis, [(b, a) for a, b in up]),
        )
    done = []
    for _, dim in sides:
        low, high = edges[dim]
        around = [(width, width) if d in done else (0, 0) for d in range(array.ndim)]
        array = jnp.concatenate([jnp.pad(low, around), array, jnp.pad(high, around)], axis=dim)
        done.append(dim)
    return array


def predict(padded):
    velocity = padded[:3]
    pressure = padded[3]
    wall_zeros = jnp.zeros(velocity.shape[:3] + (1,), jnp.float32)
    fields = jnp.concatenate([wall_zeros, velocity, wall_zeros], axis=3)
    pressure_y = jnp.concatenate([pressure[:, :, :1], pressure, pressure[:, :, -1:]], axis=2)
    centre = fields[:, 1:-1, 1:-1, 1:-1]
    x_plus = fields[:, 2:, 1:-1, 1:-1]
    x_minus = fields[:, :-2, 1:-1, 1:-1]
    z_plus = fields[:, 1:-1, 2:, 1:-1]
    z_minus = fields[:, 1:-1, :-2, 1:-1]
    y_plus = fields[:, 1:-1, 1:-1, 2:]
    y_minus = fields[:, 1:-1, 1:-1, :-2]
    laplace = x_plus + x_minus + z_plus + z_minus + y_plus + y_minus - 6.0 * centre
    advect = (
        centre[0:1] * (x_plus - x_minus)
        + centre[1:2] * (y_plus - y_minus)
        + centre[2:3] * (z_plus - z_minus)
    ) * 0.5
    gradient_x = (pressure_y[2:, 1:-1, 1:-1] - pressure_y[:-2, 1:-1, 1:-1]) * 0.5
    gradient_y = (pressure_y[1:-1, 1:-1, 2:] - pressure_y[1:-1, 1:-1, :-2]) * 0.5
    gradient_z = (pressure_y[1:-1, 2:, 1:-1] - pressure_y[1:-1, :-2, 1:-1]) * 0.5
    gradient = jnp.stack([gradient_x - drive_force, gradient_y, gradient_z])
    return centre + time_step * (viscosity * laplace - advect - gradient)


def parts(value):
    high = value.astype(jnp.bfloat16)
    return high, (value - high.astype(jnp.float32)).astype(jnp.bfloat16)


def tap_weights(length, first, taps):
    offset = lax.broadcasted_iota(jnp.int32, (length, first.shape[-1]), 0) - first
    weight = jnp.where(offset == 3, taps[3], 0.0)
    for t in (2, 1, 0):
        weight = jnp.where(offset == t, taps[t], weight)
    return weight


def dot(a, b, across):
    return lax.dot_general(
        a, b, (((1,), (across,)), ((), ())), preferred_element_type=jnp.float32
    )


def marker_kernel(
    ids, starts, moving, turning, cells, fracs, field, force, tap, cross, spread, way_y, load
):
    force[...] = jnp.zeros_like(force)
    half_pi = 0.5 * math.pi
    angle = fracs[...] * half_pi
    cosine, sine = jnp.cos(angle), jnp.sin(angle)
    tap[0] = 0.25 * (1.0 - sine)
    tap[1] = 0.25 * (1.0 + cosine)
    tap[2] = 0.25 * (1.0 + sine)
    tap[3] = 0.25 * (1.0 - cosine)
    markers = fracs.shape[2]
    wall = field.shape[3]

    def one_slot(s, carry):
        @pl.when(ids[s] >= 0)
        def _():
            n = ids[s]
            x0, y0, z0 = starts[0, s], starts[1, s], starts[2, s]
            zb = pl.multiple_of((z0 // 8) * 8, 8)
            cell = cells[s]
            frac = fracs[s]
            taps = [tap[t, s] for t in range(4)]

            def along(d):
                return [w[d : d + 1] for w in taps]

            weight_x = tap_weights(BOX, cell[0:1] - 1, along(0))
            weight_y = tap_weights(wall, cell[1:2] - 1 + y0, along(1))
            weight_z = tap_weights(BAND, cell[2:3] - 1 + (z0 - zb), along(2))
            for i in range(BOX):
                cross[i // STEP, i % STEP] = weight_x[i : i + 1] * weight_z
            spread[...] = weight_y
            y_high, y_low = parts(weight_y)
            way_y[0] = y_high
            way_y[1] = y_low

            def sample(t, total):
                window = field[:, pl.ds(x0 + t * STEP, STEP), pl.ds(zb, BAND), :]
                high, low = parts(window.reshape(3 * STEP * BAND, wall))
                value = dot(high, way_y[0], 0) + dot(low, way_y[0], 0) + dot(high, way_y[1], 0)
                value = value.reshape(3, STEP * BAND // 8, 8, markers)
                factor = cross[t].reshape(1, STEP * BAND // 8, 8, markers)
                return total + jnp.sum(value * factor, axis=1)

            total = lax.fori_loop(
                0, BOX // STEP, sample, jnp.zeros((3, 8, markers), jnp.float32)
            )
            sampled = jnp.sum(total, axis=1)
            lever = cell.astype(jnp.float32) + frac - float(HALF)
            spin = [turning[c, n] for c in range(3)]
            for c in range(3):
                a, b = (c + 1) % 3, (c + 2) % 3
                target = moving[c, n] + (spin[a] * lever[b : b + 1] - spin[b] * lever[a : a + 1])
                push = target - sampled[c : c + 1]
                high, low = parts(spread[...] * push)
                load[0, pl.ds(c * wall, wall), :] = high
                load[1, pl.ds(c * wall, wall), :] = low

            def scatter(t, carry):
                high, low = parts(cross[t].reshape(STEP * BAND, markers))
                value = dot(high, load[0], 1) + dot(low, load[0], 1) + dot(high, load[1], 1)
                for c in range(3):
                    force[c, pl.ds(x0 + t * STEP, STEP), pl.ds(zb, BAND), :] += value[
                        :, c * wall : (c + 1) * wall
                    ].reshape(STEP, BAND, wall)
                return carry

            lax.fori_loop(0, BOX // STEP, scatter, 0)

        return carry

    lax.fori_loop(0, ids.shape[0], one_slot, 0)


def spread_forces(extended, slot_ids, starts, cells, fracs, moving, turning):
    slots, _, markers = cells.shape
    wall = extended.shape[3]
    scalar = pl.BlockSpec(memory_space=pltpu.SMEM)
    vector = pl.BlockSpec(memory_space=pltpu.VMEM)
    return pl.pallas_call(
        marker_kernel,
        out_shape=jax.ShapeDtypeStruct(extended.shape, jnp.float32),
        in_specs=[scalar] * 4 + [vector] * 3,
        out_specs=vector,
        scratch_shapes=[
            pltpu.VMEM((4, slots, 3, markers), jnp.float32),
            pltpu.VMEM((BOX // STEP, STEP, BAND, markers), jnp.float32),
            pltpu.VMEM((wall, markers), jnp.float32),
            pltpu.VMEM((2, wall, markers), jnp.bfloat16),
            pltpu.VMEM((2, 3 * wall, markers), jnp.bfloat16),
        ],
        name="markers",
    )(slot_ids, starts, moving, turning, cells, fracs, extended)


def dot3(high, low, other_high, other_low):
    return dot(high, other_high, 0) + dot(low, other_high, 0) + dot(high, other_low, 0)


def exchanged(rows, lane_bits):
    lane = lax.broadcasted_iota(jnp.int32, rows[0].shape, rows[0].ndim - 1)
    axis = rows[0].ndim - 1
    for bit, shift in enumerate(lane_bits):
        low = (lane & shift) == 0
        step = 1 << bit
        out = list(rows)
        for m in range(len(rows)):
            if m & step == 0:
                a, b = rows[m], rows[m + step]
                out[m] = jnp.where(low, a, pltpu.roll(b, shift, axis))
                out[m + step] = jnp.where(low, pltpu.roll(a, 128 - shift, axis), b)
        rows = out
    return rows


def remote(source, target, sems, slot, to):
    return pltpu.make_async_remote_copy(
        src_ref=source,
        dst_ref=target,
        send_sem=sems[0].at[slot],
        recv_sem=sems[1].at[slot],
        device_id=to,
        device_id_type=MESH,
    )


def spectrum_kernel(
    nx, nz, scale, force, field, table_z, table_x, velocity, source,
    z_got, x_out, x_got, edge_u, edge_w, edge_w_out, cut, planes, modes, rows,
    z_send, z_recv, x_send, x_recv, e_send, e_recv, c_send, c_recv, m_send, m_recv,
):
    gx, gz = lax.axis_index("gx"), lax.axis_index("gz")
    below = (gx, lax.rem(gz + nz - 1, nz))
    above = (gx, lax.rem(gz + 1, nz))
    left = (lax.rem(gx + nx - 1, nx), gz)
    right = (lax.rem(gx + 1, nx), gz)
    barrier = pltpu.get_barrier_semaphore()

    def greet_z(d, carry):
        pl.semaphore_signal(
            barrier, inc=1, device_id=(gx, lax.rem(gz + d, nz)), device_id_type=MESH
        )
        return carry

    def greet_x(d, carry):
        pl.semaphore_signal(
            barrier, inc=1, device_id=(lax.rem(gx + d, nx), gz), device_id_type=MESH
        )
        return carry

    lax.fori_loop(1, nz, greet_z, 0)
    lax.fori_loop(1, nx, greet_x, 0)
    pl.semaphore_wait(barrier, nx + nz - 2)

    wide, tall = velocity.shape[1], velocity.shape[2]
    order = (0, 2, 1)
    z_copies, x_copies = {}, {}
    for c in order:
        down = remote(
            force.at[c, :, pl.ds(0, SIDE), :], z_got.at[1, c], (z_send, z_recv), (1, c), below
        )
        up = remote(
            force.at[c, :, pl.ds(SIDE + tall, SIDE), :],
            z_got.at[0, c],
            (z_send, z_recv),
            (0, c),
            above,
        )
        down.start()
        up.start()
        z_copies[c] = (down, up)
    for c in order:
        for copy in z_copies[c]:
            copy.wait_recv()
        for part in range(2):
            inner = pl.ds(part * SIDE, SIDE)
            outer = pl.ds(SIDE + part * SIDE, SIDE)
            x_out[0, c, :, inner, :] = (
                force[c, pl.ds(0, HALF), outer, :] + z_got[part, c, pl.ds(0, HALF)]
            )
            x_out[1, c, :, inner, :] = (
                force[c, pl.ds(HALF + wide, HALF), outer, :]
                + z_got[part, c, pl.ds(HALF + wide, HALF)]
            )
        back = remote(x_out.at[0, c], x_got.at[1, c], (x_send, x_recv), (1, c), left)
        ahead = remote(x_out.at[1, c], x_got.at[0, c], (x_send, x_recv), (0, c), right)
        back.start()
        ahead.start()
        x_copies[c] = (back, ahead)
        for part in range(2):
            inner = pl.ds(part * SIDE, SIDE)
            outer = pl.ds(SIDE + part * SIDE, SIDE)
            velocity[c, :, inner, :] = (
                field[c, pl.ds(HALF, wide), outer, :]
                + force[c, pl.ds(HALF, wide), outer, :]
                + z_got[part, c, pl.ds(HALF, wide)]
            )
    edges = []
    for c in order:
        for copy in x_copies[c]:
            copy.wait_recv()
        velocity[c, pl.ds(0, HALF)] += x_got[0, c]
        velocity[c, pl.ds(wide - HALF, HALF)] += x_got[1, c]
        if c == 0:
            edges += [
                remote(velocity.at[0, 0], edge_u.at[1], (e_send, e_recv), 0, left),
                remote(velocity.at[0, wide - 1], edge_u.at[0], (e_send, e_recv), 1, right),
            ]
        if c == 2:
            edge_w_out[0] = velocity[2, :, 0, :]
            edge_w_out[1] = velocity[2, :, tall - 1, :]
            edges += [
                remote(edge_w_out.at[0], edge_w.at[1], (e_send, e_recv), 2, below),
                remote(edge_w_out.at[1], edge_w.at[0], (e_send, e_recv), 3, above),
            ]
        if c != 1:
            edges[-2].start()
            edges[-1].start()
    wall = velocity.shape[3]
    lane = lax.broadcasted_iota(jnp.int32, (1, 1, wall), 2)
    normal = velocity[1]
    upper = jnp.where(lane == wall - 1, 0.0, pltpu.roll(normal, wall - 1, 2))
    lower = jnp.where(lane == 0, 0.0, pltpu.roll(normal, 1, 2))
    divergence = upper - lower
    for copy in edges:
        copy.wait_recv()
    stream = velocity[0]
    divergence += jnp.concatenate([stream[1:], edge_u[1:2]], axis=0) - jnp.concatenate(
        [edge_u[0:1], stream[:-1]], axis=0
    )
    span = velocity[2]
    row = lax.broadcasted_iota(jnp.int32, (1, tall, 1), 1)
    after = jnp.where(row == tall - 1, edge_w[1][:, None, :], pltpu.roll(span, tall - 1, 1))
    before = jnp.where(row == 0, edge_w[0][:, None, :], pltpu.roll(span, 1, 1))
    divergence = (divergence + (after - before)) * 0.5
    for half in range(wide // 8):
        blocks = exchanged([divergence[half * 8 + i] for i in range(8)], (16, 32, 64))
        for j in range(nz):
            cut[j, :, pl.ds(half * 128, 128)] = blocks[j]

    def cut_copy(d):
        to = lax.rem(gz + d, nz)
        return pltpu.make_async_remote_copy(
            src_ref=cut.at[to],
            dst_ref=planes.at[gz],
            send_sem=c_send.at[to],
            recv_sem=c_recv.at[gz],
            device_id=(gx, to),
            device_id_type=MESH,
        )

    def cut_from(d):
        origin = lax.rem(gz + d, nz)
        return pltpu.make_async_remote_copy(
            src_ref=cut.at[origin],
            dst_ref=planes.at[origin],
            send_sem=c_send.at[origin],
            recv_sem=c_recv.at[origin],
            device_id=(gx, origin),
            device_id_type=MESH,
        )

    def start(make):
        def go(d, carry):
            make(d).start()
            return carry

        return go

    def wait_recv(make):
        def go(d, carry):
            make(d).wait_recv()
            return carry

        return go

    def wait_send(make):
        def go(d, carry):
            make(d).wait_send()
            return carry

        return go

    lax.fori_loop(1, nz, start(cut_copy), 0)
    planes[gz] = cut[gz]
    lax.fori_loop(1, nz, wait_recv(cut_from), 0)
    high, low = parts(planes[...].reshape(nz * tall, 2 * 128))
    modes[...] = dot3(table_z[0], table_z[1], high, low).reshape(modes.shape)

    def mode_copy(d):
        to = lax.rem(gx + d, nx)
        return pltpu.make_async_remote_copy(
            src_ref=modes.at[:, to],
            dst_ref=rows.at[gx],
            send_sem=m_send.at[to],
            recv_sem=m_recv.at[gx],
            device_id=(to, gz),
            device_id_type=MESH,
        )

    def mode_from(d):
        origin = lax.rem(gx + d, nx)
        return pltpu.make_async_remote_copy(
            src_ref=modes.at[:, origin],
            dst_ref=rows.at[origin],
            send_sem=m_send.at[origin],
            recv_sem=m_recv.at[origin],
            device_id=(origin, gz),
            device_id_type=MESH,
        )

    lax.fori_loop(1, nx, start(mode_copy), 0)
    rows[gx] = modes[:, gx]
    lax.fori_loop(1, nx, wait_recv(mode_from), 0)
    columns = []
    for h in range(nx // 16):
        for half in range(2):
            blocks = exchanged(
                [rows[h * 16 + b, :, :, half * 128 : half * 128 + 128] for b in range(16)],
                (1, 2, 4, 8),
            )
            columns.append(
                jnp.concatenate([block[0] for block in blocks] + [block[1] for block in blocks])
            )
    high, low = parts(jnp.concatenate(columns, axis=1))
    lines = high.shape[0] // 2
    for q in range(table_x.shape[1]):
        value = dot3(high, low, table_x[0, q], table_x[1, q])
        real = value[:lines, :128] + value[lines:, 128:]
        imag = value[lines:, :128] - value[:lines, 128:]
        out = pl.ds(q * 128, 128)
        source[0, :, :, out] = (real * scale).reshape(source.shape[1], source.shape[2], 128)
        source[1, :, :, out] = (imag * scale).reshape(source.shape[1], source.shape[2], 128)
    for c in order:
        for copy in z_copies[c] + x_copies[c]:
            copy.wait_send()
    for copy in edges:
        copy.wait_send()
    lax.fori_loop(1, nz, wait_send(cut_copy), 0)
    lax.fori_loop(1, nx, wait_send(mode_copy), 0)


def split_table(table):
    high = table.astype(jnp.bfloat16)
    return np.stack([high, (table - high.astype(np.float64)).astype(jnp.bfloat16)])


def transform_tables(length_x, length_z):
    counter = np.arange(length_z)
    angle = counter[:, None] * counter[None, :] % length_z * (2 * math.pi / length_z)
    table_z = np.concatenate([np.cos(angle), -np.sin(angle)])
    h, half, i, b = np.meshgrid(
        np.arange(length_x // 256), np.arange(2), np.arange(8), np.arange(16), indexing="ij"
    )
    place = (16 * (16 * h + b) + 8 * half + i).reshape(-1)
    mode = np.arange(length_x)
    angle = place[:, None] * mode[None, :] % length_x * (2 * math.pi / length_x)
    both = np.stack([np.cos(angle), np.sin(angle)], axis=1)
    both = both.reshape(length_x, 2, length_x // 128, 128).transpose(2, 0, 1, 3)
    return split_table(table_z), split_table(both.reshape(length_x // 128, length_x, 256))


def spectrum(force, field, tile, nx, nz):
    _, wide, tall, wall = tile
    length_x, length_z = wide * nx, tall * nz
    table_z, table_x = transform_tables(length_x, length_z)
    vector = pl.BlockSpec(memory_space=pltpu.VMEM)
    dma = pltpu.SemaphoreType.DMA
    each = wall // nz
    deep = field.shape[1]
    return pl.pallas_call(
        functools.partial(spectrum_kernel, nx, nz, 1.0 / math.sqrt(length_x * length_z)),
        out_shape=(
            jax.ShapeDtypeStruct(tile, jnp.float32),
            jax.ShapeDtypeStruct((2, each, length_z // nx, length_x), jnp.float32),
        ),
        in_specs=[vector] * 4,
        out_specs=(vector, vector),
        scratch_shapes=[
            pltpu.VMEM((2, 3, deep, SIDE, wall), jnp.float32),
            pltpu.VMEM((2, 3, HALF, tall, wall), jnp.float32),
            pltpu.VMEM((2, 3, HALF, tall, wall), jnp.float32),
            pltpu.VMEM((2, tall, wall), jnp.float32),
            pltpu.VMEM((2, wide, wall), jnp.float32),
            pltpu.VMEM((2, wide, wall), jnp.float32),
            pltpu.VMEM((nz, tall, wide * each), jnp.float32),
            pltpu.VMEM((nz, tall, wide * each), jnp.float32),
            pltpu.VMEM((2, nx, length_z // nx, wide * each), jnp.float32),
            pltpu.VMEM((nx, 2, length_z // nx, wide * each), jnp.float32),
            dma((2, 3)), dma((2, 3)), dma((2, 3)), dma((2, 3)), dma((4,)), dma((4,)),
            dma((nz,)), dma((nz,)), dma((nx,)), dma((nx,)),
        ],
        compiler_params=pltpu.CompilerParams(collective_id=1, has_side_effects=True),
        name="spectrum",
    )(force, field, jnp.asarray(table_z), jnp.asarray(table_x))


def on_device(
    nx, nz, flow_state, slot_ids, corners, marker_cells, marker_frac, particle_velocity,
    particle_spin,
):
    tile_x = flow_state.shape[1]
    tile_z = flow_state.shape[2]
    ghosted = with_halo(flow_state, (("gx", 1), ("gz", 2)), 1)
    extended = padded_2(predict(ghosted), (("gx", 1, HALF), ("gz", 2, SIDE)))
    starts = jnp.stack(
        [
            (corners[0] - lax.axis_index("gx") * tile_x + HALF) % (tile_x * nx),
            corners[1],
            (corners[2] - lax.axis_index("gz") * tile_z + SIDE) % (tile_z * nz),
        ]
    )
    force = spread_forces(
        extended,
        slot_ids,
        starts,
        jnp.transpose(marker_cells, (1, 0, 2)),
        jnp.transpose(marker_frac, (1, 0, 2)),
        particle_velocity,
        particle_spin,
    )
    return spectrum(force, extended, (3,) + flow_state.shape[1:], nx, nz)


def solution(mesh):
    both = ("gx", "gz")
    placed = (
        P(None, "gx", "gz", None),
        P(both),
        P(None, both),
        P(None, both, None),
        P(None, both, None),
        P(),
        P(),
    )
    return jax.shard_map(
        functools.partial(on_device, mesh.shape["gx"], mesh.shape["gz"]),
        mesh=mesh,
        in_specs=placed,
        out_specs=(P(None, "gx", "gz", None), P(None, "gz", "gx", None)),
        check_vma=False,
    )
```

profile of v0, /device:TPU:1, one launch (start us, length us, event | category | flops | bytes accessed | tf_op | source)
XLA Modules:
  0.0 155.8 jit_solution(3483261058889188066)
XLA Ops:
  0.6 1.2 fusion.13
  1.8 2.6 %collective-permute-start.3 = (f32[4,16,1,128]{3,2,1,0:T(1,128)S(1)}, f32[4,16,1,128]{3,2,1,0:T(1,128)S(1)}, u32[]{:S(2)}, u32[]{:S(2)}) collective-permute-start(f32[4,16,1,128]{3,2,1,0:T(1,128)S(1)} %get-tuple-element.7), channel_id=1, source_target_pairs={{0,1},{1,2},{2,3},{3,4},{4,5},{5,6},{6,7},{7,0},{8,9},{9,10},{10,1... | collective-permute-start | bytes 98312 | tf_op jit(solution)/shard_map/ppermute | solution.py:46
  4.4 0.6 collective-permute-start.2
  5.0 0.9 fusion.14
  5.9 7.5 %collective-permute-start = (f32[4,1,32,128]{3,2,1,0:T(8,128)S(1)}, f32[4,1,32,128]{3,2,1,0:T(8,128)S(1)}, u32[]{:S(2)}, u32[]{:S(2)}) collective-permute-start(f32[4,1,32,128]{3,2,1,0:T(8,128)S(1)} %get-tuple-element.9), channel_id=1, source_target_pairs={{8,0},{16,8},{24,16},{32,24},{40,32},{48,40},{56,48},{64,56},{72,6... | collective-permute-start | bytes 196616 | tf_op jit(solution)/shard_map/ppermute | solution.py:47
  13.4 1.2 slice_bitcast_fusion.2
  14.7 5.2 %collective-permute-done.1 = f32[4,1,32,128]{3,2,1,0:T(8,128)S(1)} collective-permute-done((f32[4,1,32,128]{3,2,1,0:T(8,128)S(1)}, f32[4,1,32,128]{3,2,1,0:T(8,128)S(1)}, u32[]{:S(2)}, u32[]{:S(2)}) %collective-permute-start.1) | collective-permute-done | bytes 65568 | tf_op jit(solution)/shard_map/ppermute | solution.py:46
  20.0 0.2 pad_maximum_fusion.2
  20.5 0.3 fusion.9
  20.8 0.8 fusion.1
  21.9 4.8 %collective-permute-start.5 = (f32[3,12,32,128]{3,2,1,0:T(8,128)S(1)}, f32[3,12,32,128]{3,2,1,0:T(8,128)S(1)}, u32[]{:S(2)}, u32[]{:S(2)}) collective-permute-start(f32[3,12,32,128]{3,2,1,0:T(8,128)S(1)} %get-tuple-element.12), channel_id=1, source_target_pairs={{8,0},{16,8},{24,16},{32,24},{40,32},{48,40},{56,48},{64,56},{72,6... | collective-permute-start | bytes 1769480 | tf_op jit(solution)/shard_map/ppermute | solution.py:33
  26.7 10.1 %collective-permute-done.4 = f32[3,12,32,128]{3,2,1,0:T(8,128)S(1)} collective-permute-done((f32[3,12,32,128]{3,2,1,0:T(8,128)S(1)}, f32[3,12,32,128]{3,2,1,0:T(8,128)S(1)}, u32[]{:S(2)}, u32[]{:S(2)}) %collective-permute-start.4) | collective-permute-done | bytes 589856 | tf_op jit(solution)/shard_map/ppermute | solution.py:32
  37.0 1.5 fusion.12
  38.5 5.2 %collective-permute-start.6 = (f32[3,40,16,128]{3,2,1,0:T(8,128)}, f32[3,40,16,128]{3,2,1,0:T(8,128)S(1)}, u32[]{:S(2)}, u32[]{:S(2)}) collective-permute-start(f32[3,40,16,128]{3,2,1,0:T(8,128)} %get-tuple-element.2), channel_id=1, source_target_pairs={{0,1},{1,2},{2,3},{3,4},{4,5},{5,6},{6,7},{7,0},{8,9},{9,10},{10,1... | collective-permute-start | bytes 2949128 | tf_op jit(solution)/shard_map/ppermute | solution.py:32
  43.7 0.7 copy.16
  44.4 0.7 copy.15
  45.1 0.6 pad_add_fusion.starts
  45.7 9.4 %collective-permute-done.6 = f32[3,40,16,128]{3,2,1,0:T(8,128)S(1)} collective-permute-done((f32[3,40,16,128]{3,2,1,0:T(8,128)}, f32[3,40,16,128]{3,2,1,0:T(8,128)S(1)}, u32[]{:S(2)}, u32[]{:S(2)}) %collective-permute-start.6) | collective-permute-done | bytes 983072 | tf_op jit(solution)/shard_map/ppermute | solution.py:32
  55.1 2.5 %collective-permute-done.7 = f32[3,40,16,128]{3,2,1,0:T(8,128)} collective-permute-done((f32[3,40,16,128]{3,2,1,0:T(8,128)}, f32[3,40,16,128]{3,2,1,0:T(8,128)}, u32[]{:S(2)}, u32[]{:S(2)}) %collective-permute-start.7) | collective-permute-done | bytes 983072 | tf_op jit(solution)/shard_map/ppermute | solution.py:33
  57.6 3.5 %pad_maximum_fusion.field = f32[3,40,64,128]{3,2,1,0:T(8,128)} fusion(f32[3,40,16,128]{3,2,1,0:T(8,128)} %collective-permute-done.7, f32[3,12,32,128]{3,2,1,0:T(8,128)S(1)} %collective-permute-done.5, f32[3,16,32,128]{3,2,1,0:T(8,128)S(1)} %fusion.1, f32[3,12,32,128]{3,2,1,0:T(8,128)S(1)} %collective-permute-done.4, ...), kind=kLoop, calls=%fused_computation | loop fusion | flops 3932160 | bytes 7864320 | tf_op jit(solution)/shard_map/concatenate | solution.py:34
  61.1 31.7 %markers.1.force = f32[3,40,64,128]{3,2,1,0:T(8,128)} custom-call(s32[8]{0:T(128)} %ids.1, s32[3,8]{1,0:T(4,128)} %pad_add_fusion.starts, f32[3,1024]{1,0:T(4,128)} %moving.1, f32[3,1024]{1,0:T(4,128)} %turning.1, s32[8,3,512]{2,1,0:T(4,128)} %bitcast.20, f32[8,3,512]{2,1,0:T(4,128)} %bitcast.21, f32[3,40,64,128]{3,2,1,0:T(8,128)} %pad_maximum_fusion.field), custom_call_target="tpu_custom_call" | custom-call | tf_op jit(solution)/shard_map/markers/pallas_call | solution.py:183
  92.7 59.1 %spectrum.1 = (f32[3,16,32,128]{3,2,1,0:T(8,128)}, f32[2,16,8,512]{3,2,1,0:T(8,128)}) custom-call(f32[3,40,64,128]{3,2,1,0:T(8,128)} %markers.1.force, f32[3,40,64,128]{3,2,1,0:T(8,128)} %pad_maximum_fusion.field, bf16[2,512,256]{2,1,0:T(8,128)(2,1)} %constant.62.clone.table_z, bf16[2,4,512,256]{3,2,1,0:T(8,128)(2,1)} %constant.63.clone.table_x), custom_call_target="tpu_custom_call" | custom-call | tf_op jit(solution)/shard_map/spectrum/pallas_call | solution.py:474
  151.8 2.1 %copy.21 = f32[3,16,32,128]{3,2,1,0:T(8,128)} copy(f32[3,16,32,128]{3,2,1,0:T(8,128)} %get-tuple-element.23) | data formatting | bytes 1572864
  153.9 1.9 %copy.22 = f32[2,16,8,512]{3,2,1,0:T(8,128)} copy(f32[2,16,8,512]{3,2,1,0:T(8,128)} %get-tuple-element.24) | data formatting | bytes 1048576
  (26 shorter events, 0.9 us)
Async XLA Ops:
  0.6 19.2 %copy-start = (f32[4,16,32,128]{3,2,1,0:T(8,128)S(1)}, f32[4,16,32,128]{3,2,1,0:T(8,128)}, u32[]{:S(2)}) copy-start(f32[4,16,32,128]{3,2,1,0:T(8,128)} %param.9) | copy-start | bytes 3145732
  1.8 12.8 %collective-permute-start.3 = (f32[4,16,1,128]{3,2,1,0:T(1,128)S(1)}, f32[4,16,1,128]{3,2,1,0:T(1,128)S(1)}, u32[]{:S(2)}, u32[]{:S(2)}) collective-permute-start(f32[4,16,1,128]{3,2,1,0:T(1,128)S(1)} %get-tuple-element.7), channel_id=1, source_target_pairs={{0,1},{1,2},{2,3},{3,4},{4,5},{5,6},{6,7},{7,0},{8,9},{9,10},{10,1... | collective-permute-start | bytes 98312 | tf_op jit(solution)/shard_map/ppermute | solution.py:46
  4.4 10.2 %collective-permute-start.2 = (f32[4,16,1,128]{3,2,1,0:T(1,128)S(1)}, f32[4,16,1,128]{3,2,1,0:T(1,128)S(1)}, u32[]{:S(2)}, u32[]{:S(2)}) collective-permute-start(f32[4,16,1,128]{3,2,1,0:T(1,128)S(1)} %get-tuple-element.8), channel_id=1, source_target_pairs={{1,0},{2,1},{3,2},{4,3},{5,4},{6,5},{7,6},{0,7},{9,8},{10,9},{11,1... | collective-permute-start | bytes 98312 | tf_op jit(solution)/shard_map/ppermute | solution.py:47
  5.9 14.0 %collective-permute-start = (f32[4,1,32,128]{3,2,1,0:T(8,128)S(1)}, f32[4,1,32,128]{3,2,1,0:T(8,128)S(1)}, u32[]{:S(2)}, u32[]{:S(2)}) collective-permute-start(f32[4,1,32,128]{3,2,1,0:T(8,128)S(1)} %get-tuple-element.9), channel_id=1, source_target_pairs={{8,0},{16,8},{24,16},{32,24},{40,32},{48,40},{56,48},{64,56},{72,6... | collective-permute-start | bytes 196616 | tf_op jit(solution)/shard_map/ppermute | solution.py:47
  13.4 6.4 %collective-permute-start.1 = (f32[4,1,32,128]{3,2,1,0:T(8,128)S(1)}, f32[4,1,32,128]{3,2,1,0:T(8,128)S(1)}, u32[]{:S(2)}, u32[]{:S(2)}) collective-permute-start(f32[4,1,32,128]{3,2,1,0:T(8,128)S(1)} %get-tuple-element.10), channel_id=1, source_target_pairs={{0,8},{8,16},{16,24},{24,32},{32,40},{40,48},{48,56},{56,64},{64,7... | collective-permute-start | bytes 196616 | tf_op jit(solution)/shard_map/ppermute | solution.py:46
  21.8 15.0 %collective-permute-start.4 = (f32[3,12,32,128]{3,2,1,0:T(8,128)S(1)}, f32[3,12,32,128]{3,2,1,0:T(8,128)S(1)}, u32[]{:S(2)}, u32[]{:S(2)}) collective-permute-start(f32[3,12,32,128]{3,2,1,0:T(8,128)S(1)} %get-tuple-element.11), channel_id=1, source_target_pairs={{0,8},{8,16},{16,24},{24,32},{32,40},{40,48},{48,56},{56,64},{64,7... | collective-permute-start | bytes 1769480 | tf_op jit(solution)/shard_map/ppermute | solution.py:32
  21.9 14.9 %collective-permute-start.5 = (f32[3,12,32,128]{3,2,1,0:T(8,128)S(1)}, f32[3,12,32,128]{3,2,1,0:T(8,128)S(1)}, u32[]{:S(2)}, u32[]{:S(2)}) collective-permute-start(f32[3,12,32,128]{3,2,1,0:T(8,128)S(1)} %get-tuple-element.12), channel_id=1, source_target_pairs={{8,0},{16,8},{24,16},{32,24},{40,32},{48,40},{56,48},{64,56},{72,6... | collective-permute-start | bytes 1769480 | tf_op jit(solution)/shard_map/ppermute | solution.py:33
  37.0 6.8 %copy-start.1 = (s32[3,8,512]{2,1,0:T(8,128)S(1)}, s32[3,8,512]{2,1,0:T(8,128)}, u32[]{:S(2)}) copy-start(s32[3,8,512]{2,1,0:T(8,128)} %param.12) | copy-start | bytes 147460
  37.0 7.4 %copy-start.2 = (f32[3,8,512]{2,1,0:T(8,128)S(1)}, f32[3,8,512]{2,1,0:T(8,128)}, u32[]{:S(2)}) copy-start(f32[3,8,512]{2,1,0:T(8,128)} %param.13) | copy-start | bytes 147460
  37.0 8.1 %copy-start.3 = (s32[3,8]{1,0:T(4,128)S(1)}, s32[3,8]{1,0:T(4,128)}, u32[]{:S(2)}) copy-start(s32[3,8]{1,0:T(4,128)} %param.11) | copy-start | bytes 292
  38.5 16.6 %collective-permute-start.6 = (f32[3,40,16,128]{3,2,1,0:T(8,128)}, f32[3,40,16,128]{3,2,1,0:T(8,128)S(1)}, u32[]{:S(2)}, u32[]{:S(2)}) collective-permute-start(f32[3,40,16,128]{3,2,1,0:T(8,128)} %get-tuple-element.2), channel_id=1, source_target_pairs={{0,1},{1,2},{2,3},{3,4},{4,5},{5,6},{6,7},{7,0},{8,9},{9,10},{10,1... | collective-permute-start | bytes 2949128 | tf_op jit(solution)/shard_map/ppermute | solution.py:32
  43.7 13.8 %collective-permute-start.7 = (f32[3,40,16,128]{3,2,1,0:T(8,128)}, f32[3,40,16,128]{3,2,1,0:T(8,128)}, u32[]{:S(2)}, u32[]{:S(2)}) collective-permute-start(f32[3,40,16,128]{3,2,1,0:T(8,128)} %get-tuple-element.3), channel_id=1, source_target_pairs={{1,0},{2,1},{3,2},{4,3},{5,4},{6,5},{7,6},{0,7},{9,8},{10,9},{11,1... | collective-permute-start | bytes 2949128 | tf_op jit(solution)/shard_map/ppermute | solution.py:33
where the time goes:
time: 157 us; the launch traced here: 156 us
  Pallas kernels  90.7 us (58%)
  waiting for transfers between devices  27.2 us (17%)
  starting transfers between devices  20.8 us (13%)
  local copies, waits for them, and re-layouts  10.5 us (7%)
  other arithmetic  5.68 us (4%)
    pallas_call x1, Pallas kernels, spectrum(): pl.pallas_call(functools.partial(spectrum_kernel, nx, nz, 1.0 / math.sqrt...  59.1 us
    pallas_call x1, Pallas kernels, spread_forces(): pl.pallas_call(marker_kernel, out_shape=jax.ShapeDtypeStruct(extended.sha...  31.7 us
    ppermute x2, waiting for transfers between devices, padded_2(): before = lax.ppermute(last, axis, up)  19.5 us
    ppermute x2, starting transfers between devices, with_halo(): lax.ppermute(first, axis, [(b, a) for a, b in up])  8.11 us
    unnamed x14, local copies, waits for them, and re-layouts  5.37 us
    ppermute x2, starting transfers between devices, padded_2(): before = lax.ppermute(last, axis, up)  5.32 us
    ppermute x2, waiting for transfers between devices, with_halo(): lax.ppermute(last, axis, up)  5.18 us
    ppermute x2, starting transfers between devices, padded_2(): after = lax.ppermute(first, axis, down)  4.78 us
  transfers between devices with their start and end apart: 8, of which 4 were waited for; matrix products, arithmetic and copies ran while one was open for 3% of the time, Pallas kernels for 0%

commit v1 on v0

--- a/solution.py
+++ b/solution.py
@@ -22,63 +22,165 @@
 drive_force = 1.0
 
 
-def padded_2(array, sides):
-    for axis, dim, width in sides:
-        devices, length = (lax.axis_size(axis), array.shape[dim])
-        up = [(i, (i + 1) % devices) for i in range(devices)]
-        down = [(j, i) for i, j in up]
-        last = lax.slice_in_dim(array, length - width, length, axis=dim)
-        first = lax.slice_in_dim(array, 0, width, axis=dim)
-        before = lax.ppermute(last, axis, up)
-        after = lax.ppermute(first, axis, down)
-        array = jnp.concatenate([before, array, after], axis=dim)
-    return array
-
-
-def with_halo(array, sides, width):
-    edges = {}
-    for axis, dim in sides:
-        devices, length = (lax.axis_size(axis), array.shape[dim])
-        up = [(i, (i + 1) % devices) for i in range(devices)]
-        last = lax.slice_in_dim(array, length - width, length, axis=dim)
-        first = lax.slice_in_dim(array, 0, width, axis=dim)
-        edges[dim] = (
-            lax.ppermute(last, axis, up),
-            lax.ppermute(first, axis, [(b, a) for a, b in up]),
-        )
-    done = []
-    for _, dim in sides:
-        low, high = edges[dim]
-        around = [(width, width) if d in done else (0, 0) for d in range(array.ndim)]
-        array = jnp.concatenate([jnp.pad(low, around), array, jnp.pad(high, around)], axis=dim)
-        done.append(dim)
-    return array
-
-
-def predict(padded):
-    velocity = padded[:3]
-    pressure = padded[3]
-    wall_zeros = jnp.zeros(velocity.shape[:3] + (1,), jnp.float32)
-    fields = jnp.concatenate([wall_zeros, velocity, wall_zeros], axis=3)
-    pressure_y = jnp.concatenate([pressure[:, :, :1], pressure, pressure[:, :, -1:]], axis=2)
-    centre = fields[:, 1:-1, 1:-1, 1:-1]
-    x_plus = fields[:, 2:, 1:-1, 1:-1]
-    x_minus = fields[:, :-2, 1:-1, 1:-1]
-    z_plus = fields[:, 1:-1, 2:, 1:-1]
-    z_minus = fields[:, 1:-1, :-2, 1:-1]
-    y_plus = fields[:, 1:-1, 1:-1, 2:]
-    y_minus = fields[:, 1:-1, 1:-1, :-2]
-    laplace = x_plus + x_minus + z_plus + z_minus + y_plus + y_minus - 6.0 * centre
-    advect = (
-        centre[0:1] * (x_plus - x_minus)
-        + centre[1:2] * (y_plus - y_minus)
-        + centre[2:3] * (z_plus - z_minus)
-    ) * 0.5
-    gradient_x = (pressure_y[2:, 1:-1, 1:-1] - pressure_y[:-2, 1:-1, 1:-1]) * 0.5
-    gradient_y = (pressure_y[1:-1, 1:-1, 2:] - pressure_y[1:-1, 1:-1, :-2]) * 0.5
-    gradient_z = (pressure_y[1:-1, 2:, 1:-1] - pressure_y[1:-1, :-2, 1:-1]) * 0.5
-    gradient = jnp.stack([gradient_x - drive_force, gradient_y, gradient_z])
-    return centre + time_step * (viscosity * laplace - advect - gradient)
+def remote(source, target, sems, slot, to):
+    return pltpu.make_async_remote_copy(
+        src_ref=source,
+        dst_ref=target,
+        send_sem=sems[0].at[slot],
+        recv_sem=sems[1].at[slot],
+        device_id=to,
+        device_id_type=MESH,
+    )
+
+
+def around(nx, nz):
+    gx, gz = lax.axis_index("gx"), lax.axis_index("gz")
+    return (
+        (lax.rem(gx + nx - 1, nx), gz),
+        (lax.rem(gx + 1, nx), gz),
+        (gx, lax.rem(gz + nz - 1, nz)),
+        (gx, lax.rem(gz + 1, nz)),
+    )
+
+
+def front_kernel(
+    nx, nz, flow, field, edge_x, edge_z_out, edge_z,
+    e_send, e_recv, x_send, x_recv, z_send, z_recv,
+):
+    _, wide, tall, wall = flow.shape
+    left, right, below, above = around(nx, nz)
+    barrier = pltpu.get_barrier_semaphore()
+    for near in (left, right, below, above):
+        pl.semaphore_signal(barrier, inc=1, device_id=near, device_id_type=MESH)
+    pl.semaphore_wait(barrier, 4)
+    edge_z_out[0] = flow[:, :, 0, :]
+    edge_z_out[1] = flow[:, :, tall - 1, :]
+    edges = [
+        remote(flow.at[:, 0], edge_x.at[1], (e_send, e_recv), 0, left),
+        remote(flow.at[:, wide - 1], edge_x.at[0], (e_send, e_recv), 1, right),
+        remote(edge_z_out.at[0], edge_z.at[1], (e_send, e_recv), 2, below),
+        remote(edge_z_out.at[1], edge_z.at[0], (e_send, e_recv), 3, above),
+    ]
+    for copy in edges:
+        copy.start()
+    spread = time_step * viscosity
+    carry_by = 0.5 * time_step
+    lane = lax.broadcasted_iota(jnp.int32, (tall, wall), 1)
+    row = lax.broadcasted_iota(jnp.int32, (tall, wall), 0)
+    first_y, last_y = lane == 0, lane == wall - 1
+    first_z, last_z = row == 0, row == tall - 1
+
+    def layer(x, back, ahead):
+        here = [flow[c, x] for c in range(4)]
+        moves = [carry_by * here[d] for d in range(3)]
+        for c in range(3):
+            f = here[c]
+            total = f * (1.0 - 6.0 * spread)
+            y_plus = jnp.where(last_y, 0.0, pltpu.roll(f, wall - 1, 1))
+            y_minus = jnp.where(first_y, 0.0, pltpu.roll(f, 1, 1))
+            z_plus = jnp.where(last_z, 0.0, pltpu.roll(f, tall - 1, 0))
+            z_minus = jnp.where(first_z, 0.0, pltpu.roll(f, 1, 0))
+            for plus, minus, move in (
+                (ahead[c], back[c], moves[0]),
+                (y_plus, y_minus, moves[1]),
+                (z_plus, z_minus, moves[2]),
+            ):
+                total += plus * (spread - move) + minus * (spread + move)
+            p = here[3]
+            if c == 0:
+                total += time_step * drive_force - carry_by * (ahead[3] - back[3])
+            if c == 1:
+                p_plus = jnp.where(last_y, p, pltpu.roll(p, wall - 1, 1))
+                p_minus = jnp.where(first_y, p, pltpu.roll(p, 1, 1))
+                total -= carry_by * (p_plus - p_minus)
+            if c == 2:
+                p_plus = jnp.where(last_z, 0.0, pltpu.roll(p, tall - 1, 0))
+                p_minus = jnp.where(first_z, 0.0, pltpu.roll(p, 1, 0))
+                total -= carry_by * (p_plus - p_minus)
+            field[c, HALF + x, pl.ds(SIDE, tall), :] = total
+
+    def inside(x, carry):
+        layer(x, [flow[c, x - 1] for c in range(4)], [flow[c, x + 1] for c in range(4)])
+        return carry
+
+    lax.fori_loop(1, wide - 1, inside, 0)
+    for copy in edges:
+        copy.wait_recv()
+    layer(0, [edge_x[0, c] for c in range(4)], [flow[c, 1] for c in range(4)])
+    layer(
+        wide - 1, [flow[c, wide - 2] for c in range(4)], [edge_x[1, c] for c in range(4)]
+    )
+    own = pl.ds(HALF, wide)
+    x_copies, z_copies = [], []
+    for c in range(3):
+        for side, z, sign in ((0, 0, 1.0), (1, tall - 1, -1.0)):
+            move = carry_by * edge_z_out[side, 2]
+            add = edge_z[side, c] * (spread + sign * move)
+            if c == 2:
+                add += sign * carry_by * edge_z[side, 3]
+            field[c, own, SIDE + z, :] += add
+        inner = pl.ds(SIDE, tall)
+        back = remote(
+            field.at[c, pl.ds(HALF, HALF), inner],
+            field.at[c, pl.ds(HALF + wide, HALF), inner],
+            (x_send, x_recv), (0, c), left,
+        )
+        ahead = remote(
+            field.at[c, pl.ds(wide, HALF), inner],
+            field.at[c, pl.ds(0, HALF), inner],
+            (x_send, x_recv), (1, c), right,
+        )
+        back.start()
+        ahead.start()
+        x_copies.append((back, ahead))
+
+    def slabs(c, piece, columns):
+        down = remote(
+            field.at[c, columns, pl.ds(SIDE, SIDE)],
+            field.at[c, columns, pl.ds(SIDE + tall, SIDE)],
+            (z_send, z_recv), (0, c, piece), below,
+        )
+        up = remote(
+            field.at[c, columns, pl.ds(tall, SIDE)],
+            field.at[c, columns, pl.ds(0, SIDE)],
+            (z_send, z_recv), (1, c, piece), above,
+        )
+        down.start()
+        up.start()
+        z_copies.extend((down, up))
+
+    for c in range(3):
+        slabs(c, 0, own)
+    for c in range(3):
+        x_copies[c][0].wait_recv()
+        slabs(c, 1, pl.ds(HALF + wide, HALF))
+        x_copies[c][1].wait_recv()
+        slabs(c, 2, pl.ds(0, HALF))
+    for copy in z_copies:
+        copy.wait_recv()
+    for copy in edges + z_copies + [copy for pair in x_copies for copy in pair]:
+        copy.wait_send()
+
+
+def predict(flow, nx, nz):
+    _, wide, tall, wall = flow.shape
+    dma = pltpu.SemaphoreType.DMA
+    return pl.pallas_call(
+        functools.partial(front_kernel, nx, nz),
+        out_shape=jax.ShapeDtypeStruct(
+            (3, wide + 2 * HALF, tall + 2 * SIDE, wall), jnp.float32
+        ),
+        in_specs=[pl.BlockSpec(memory_space=pltpu.VMEM)],
+        out_specs=pl.BlockSpec(memory_space=pltpu.VMEM),
+        scratch_shapes=[
+            pltpu.VMEM((2, 4, tall, wall), jnp.float32),
+            pltpu.VMEM((2, 4, wide, wall), jnp.float32),
+            pltpu.VMEM((2, 4, wide, wall), jnp.float32),
+            dma((4,)), dma((4,)), dma((2, 3)), dma((2, 3)), dma((2, 3, 3)), dma((2, 3, 3)),
+        ],
+        compiler_params=pltpu.CompilerParams(collective_id=0, has_side_effects=True),
+        name="front",
+    )(flow)
 
 
 def parts(value):
@@ -120,9 +222,9 @@
             n = ids[s]
             x0, y0, z0 = starts[0, s], starts[1, s], starts[2, s]
             zb = pl.multiple_of((z0 // 8) * 8, 8)
-            cell = cells[s]
-            frac = fracs[s]
-            taps = [tap[t, s] for t in range(4)]
+            cell = cells[:, pl.ds(s, 1), :].reshape(3, markers)
+            frac = fracs[:, pl.ds(s, 1), :].reshape(3, markers)
+            taps = [tap[t, :, pl.ds(s, 1), :].reshape(3, markers) for t in range(4)]
 
             def along(d):
                 return [w[d : d + 1] for w in taps]
@@ -176,7 +278,7 @@
 
 
 def spread_forces(extended, slot_ids, starts, cells, fracs, moving, turning):
-    slots, _, markers = cells.shape
+    _, slots, markers = cells.shape
     wall = extended.shape[3]
     scalar = pl.BlockSpec(memory_space=pltpu.SMEM)
     vector = pl.BlockSpec(memory_space=pltpu.VMEM)
@@ -186,7 +288,7 @@
         in_specs=[scalar] * 4 + [vector] * 3,
         out_specs=vector,
         scratch_shapes=[
-            pltpu.VMEM((4, slots, 3, markers), jnp.float32),
+            pltpu.VMEM((4, 3, slots, markers), jnp.float32),
             pltpu.VMEM((BOX // STEP, STEP, BAND, markers), jnp.float32),
             pltpu.VMEM((wall, markers), jnp.float32),
             pltpu.VMEM((2, wall, markers), jnp.bfloat16),
@@ -214,17 +316,6 @@
                 out[m + step] = jnp.where(low, pltpu.roll(a, 128 - shift, axis), b)
         rows = out
     return rows
-
-
-def remote(source, target, sems, slot, to):
-    return pltpu.make_async_remote_copy(
-        src_ref=source,
-        dst_ref=target,
-        send_sem=sems[0].at[slot],
-        recv_sem=sems[1].at[slot],
-        device_id=to,
-        device_id_type=MESH,
-    )
 
 
 def spectrum_kernel(
@@ -504,8 +595,7 @@
 ):
     tile_x = flow_state.shape[1]
     tile_z = flow_state.shape[2]
-    ghosted = with_halo(flow_state, (("gx", 1), ("gz", 2)), 1)
-    extended = padded_2(predict(ghosted), (("gx", 1, HALF), ("gz", 2, SIDE)))
+    extended = predict(flow_state, nx, nz)
     starts = jnp.stack(
         [
             (corners[0] - lax.axis_index("gx") * tile_x + HALF) % (tile_x * nx),
@@ -517,8 +607,8 @@
         extended,
         slot_ids,
         starts,
-        jnp.transpose(marker_cells, (1, 0, 2)),
-        jnp.transpose(marker_frac, (1, 0, 2)),
+        marker_cells,
+        marker_frac,
         particle_velocity,
         particle_spin,
     )

time: 157 us -> 135 us (0.86); the launches traced: 156 us -> 136 us
  Pallas kernels: 90.7 us -> 130 us
  waiting for transfers between devices: 27.2 us -> 0 us
  starting transfers between devices: 20.8 us -> 0 us
  local copies, waits for them, and re-layouts: 10.5 us -> 3.93 us
  other arithmetic: 5.68 us -> 1.39 us
    pallas_call x0 -> x1, Pallas kernels: none -> 36.8 us  [predict(): pl.pallas_call(functools.partial(front_kernel, nx, nz), out_shape=jax.Sha...]
    ppermute x8 -> x0, waiting for transfers between devices: 27.2 us -> none  [the longest x2 19.5 us: padded_2(): before = lax.ppermute(last, axis, up)]
    ppermute x8 -> x0, starting transfers between devices: 20.8 us -> none  [the longest x2 8.11 us: with_halo(): lax.ppermute(first, axis, [(b, a) for a, b in up])]
    pallas_call x1, Pallas kernels: 59.1 us -> 65.8 us  [spectrum(): pl.pallas_call(functools.partial(spectrum_kernel, nx, nz, 1.0 / math.sqrt...]
    pallas_call x1, Pallas kernels: 31.7 us -> 27.1 us  [spread_forces(): pl.pallas_call(marker_kernel, out_shape=jax.ShapeDtypeStruct(extended.sha...]
    slice x6 -> x0, local copies, waits for them, and re-layouts: 3.92 us -> none  [the longest x2 1.62 us: padded_2(): last = lax.slice_in_dim(array, length - width, length, axis=dim)]
    concatenate x3 -> x0, other arithmetic: 3.92 us -> none  [the longest x2 3.67 us: padded_2(): array = jnp.concatenate([before, array, after], axis=dim)]
    unnamed x14 -> x2, local copies, waits for them, and re-layouts: 5.37 us -> 3.93 us
  transfers between devices with their start and end apart: 8 -> 0, of which waited for: 4 -> 0; matrix products, arithmetic and copies ran while one was open for 3% -> 0% of each run, Pallas kernels for 0% -> 0%
where the time goes in v1:
time: 135 us; the launch traced here: 136 us
  Pallas kernels  130 us (96%)
  local copies, waits for them, and re-layouts  3.93 us (3%)
  other arithmetic  1.39 us (1%)
    pallas_call x1, Pallas kernels, spectrum(): pl.pallas_call(functools.partial(spectrum_kernel, nx, nz, 1.0 / math.sqrt...  65.8 us
    pallas_call x1, Pallas kernels, predict(): pl.pallas_call(functools.partial(front_kernel, nx, nz), out_shape=jax.Sha...  36.8 us
    pallas_call x1, Pallas kernels, spread_forces(): pl.pallas_call(marker_kernel, out_shape=jax.ShapeDtypeStruct(extended.sha...  27.1 us
    unnamed x2, local copies, waits for them, and re-layouts  3.93 us

profile of v1, /device:TPU:1, one launch (start us, length us, event | category | flops | bytes accessed | tf_op | source)
XLA Modules:
  0.0 135.7 jit_solution(9687485415168834689)
XLA Ops:
  0.6 0.8 and_select_fusion.1
  1.4 0.6 pad_add_fusion.starts
  2.0 36.8 %front.1.field = f32[3,40,64,128]{3,2,1,0:T(8,128)} custom-call(f32[4,16,32,128]{3,2,1,0:T(8,128)} %flow.1), custom_call_target="tpu_custom_call" | custom-call | tf_op jit(solution)/shard_map/front/pallas_call | solution.py:168
  38.8 27.1 %markers.1.force = f32[3,40,64,128]{3,2,1,0:T(8,128)} custom-call(s32[8]{0:T(128)} %ids.1, s32[3,8]{1,0:T(4,128)} %pad_add_fusion.starts, f32[3,1024]{1,0:T(4,128)} %moving.1, f32[3,1024]{1,0:T(4,128)} %turning.1, s32[3,8,512]{2,1,0:T(8,128)} %cells.1, f32[3,8,512]{2,1,0:T(8,128)} %fracs.1, f32[3,40,64,128]{3,2,1,0:T(8,128)} %front.1.field), custom_call_target="tpu_custom_call" | custom-call | tf_op jit(solution)/shard_map/markers/pallas_call | solution.py:285
  65.9 65.8 %spectrum.1 = (f32[3,16,32,128]{3,2,1,0:T(8,128)}, f32[2,16,8,512]{3,2,1,0:T(8,128)}) custom-call(f32[3,40,64,128]{3,2,1,0:T(8,128)} %markers.1.force, f32[3,40,64,128]{3,2,1,0:T(8,128)} %front.1.field, bf16[2,512,256]{2,1,0:T(8,128)(2,1)} %constant.46.clone.table_z, bf16[2,4,512,256]{3,2,1,0:T(8,128)(2,1)} %constant.47.clone.table_x), custom_call_target="tpu_custom_call" | custom-call | tf_op jit(solution)/shard_map/spectrum/pallas_call | solution.py:565
  131.7 2.1 %copy.13 = f32[3,16,32,128]{3,2,1,0:T(8,128)} copy(f32[3,16,32,128]{3,2,1,0:T(8,128)} %get-tuple-element.7) | data formatting | bytes 1572864
  133.8 1.9 %copy.14 = f32[2,16,8,512]{3,2,1,0:T(8,128)} copy(f32[2,16,8,512]{3,2,1,0:T(8,128)} %get-tuple-element.8) | data formatting | bytes 1048576

commit v2 on v1

--- a/solution.py
+++ b/solution.py
@@ -12,7 +12,6 @@
 BOX = 24
 HALF = 12
 BAND = 32
-STEP = 8
 SIDE = 16
 MESH = pl.DeviceIdType.MESH
 
@@ -178,7 +177,9 @@
             pltpu.VMEM((2, 4, wide, wall), jnp.float32),
             dma((4,)), dma((4,)), dma((2, 3)), dma((2, 3)), dma((2, 3, 3)), dma((2, 3, 3)),
         ],
-        compiler_params=pltpu.CompilerParams(collective_id=0, has_side_effects=True),
+        compiler_params=pltpu.CompilerParams(
+            collective_id=0, has_side_effects=True, vmem_limit_bytes=12 << 20
+        ),
         name="front",
     )(flow)
 
@@ -202,8 +203,14 @@
     )
 
 
+def pair(a, b, across):
+    rows = a[0].shape[0]
+    both = dot(jnp.concatenate(a), b[0], across)
+    return both[:rows] + both[rows:] + dot(a[0], b[1], across)
+
+
 def marker_kernel(
-    ids, starts, moving, turning, cells, fracs, field, force, tap, cross, spread, way_y, load
+    nx, nz, ids, corners, moving, turning, cells, fracs, field, force, tap, cross
 ):
     force[...] = jnp.zeros_like(force)
     half_pi = 0.5 * math.pi
@@ -215,12 +222,19 @@
     tap[3] = 0.25 * (1.0 - cosine)
     markers = fracs.shape[2]
     wall = field.shape[3]
+    wide, tall = field.shape[1] - 2 * HALF, field.shape[2] - 2 * SIDE
+    first_x = lax.axis_index("gx") * wide - HALF
+    first_z = lax.axis_index("gz") * tall - SIDE
+    many = wall // BAND
+    lane = lax.broadcasted_iota(jnp.int32, (1, 1, wall), 2)
 
     def one_slot(s, carry):
         @pl.when(ids[s] >= 0)
         def _():
             n = ids[s]
-            x0, y0, z0 = starts[0, s], starts[1, s], starts[2, s]
+            x0 = lax.rem(corners[0, s] - first_x + wide * nx, wide * nx)
+            y0 = corners[1, s]
+            z0 = lax.rem(corners[2, s] - first_z + tall * nz, tall * nz)
             zb = pl.multiple_of((z0 // 8) * 8, 8)
             cell = cells[:, pl.ds(s, 1), :].reshape(3, markers)
             frac = fracs[:, pl.ds(s, 1), :].reshape(3, markers)
@@ -230,72 +244,60 @@
                 return [w[d : d + 1] for w in taps]
 
             weight_x = tap_weights(BOX, cell[0:1] - 1, along(0))
-            weight_y = tap_weights(wall, cell[1:2] - 1 + y0, along(1))
+            weight_y = tap_weights(BAND, cell[1:2] - 1, along(1))
             weight_z = tap_weights(BAND, cell[2:3] - 1 + (z0 - zb), along(2))
             for i in range(BOX):
-                cross[i // STEP, i % STEP] = weight_x[i : i + 1] * weight_z
-            spread[...] = weight_y
-            y_high, y_low = parts(weight_y)
-            way_y[0] = y_high
-            way_y[1] = y_low
-
-            def sample(t, total):
-                window = field[:, pl.ds(x0 + t * STEP, STEP), pl.ds(zb, BAND), :]
-                high, low = parts(window.reshape(3 * STEP * BAND, wall))
-                value = dot(high, way_y[0], 0) + dot(low, way_y[0], 0) + dot(high, way_y[1], 0)
-                value = value.reshape(3, STEP * BAND // 8, 8, markers)
-                factor = cross[t].reshape(1, STEP * BAND // 8, 8, markers)
-                return total + jnp.sum(value * factor, axis=1)
-
-            total = lax.fori_loop(
-                0, BOX // STEP, sample, jnp.zeros((3, 8, markers), jnp.float32)
-            )
-            sampled = jnp.sum(total, axis=1)
+                high, low = parts(weight_x[i : i + 1] * weight_y)
+                cross[0, pl.ds(i * BAND, BAND), :] = high
+                cross[1, pl.ds(i * BAND, BAND), :] = low
+            columns = []
+            for q in range(BOX // many):
+                packed = None
+                for r in range(many):
+                    piece = field[:, x0 + (q * many + r), pl.ds(zb, BAND), :]
+                    piece = pltpu.roll(piece, lax.rem(wall + r * BAND - y0, wall), 2)
+                    packed = piece if r == 0 else jnp.where(lane < r * BAND, packed, piece)
+                columns.append(packed.reshape(3 * BAND, wall))
+            window = parts(jnp.concatenate(columns, axis=1))
+            value = pair(window, (cross[0], cross[1]), 0).reshape(3, BAND, markers)
+            sampled = jnp.sum(value * weight_z[None], axis=1)
             lever = cell.astype(jnp.float32) + frac - float(HALF)
             spin = [turning[c, n] for c in range(3)]
+            loads = []
             for c in range(3):
                 a, b = (c + 1) % 3, (c + 2) % 3
                 target = moving[c, n] + (spin[a] * lever[b : b + 1] - spin[b] * lever[a : a + 1])
-                push = target - sampled[c : c + 1]
-                high, low = parts(spread[...] * push)
-                load[0, pl.ds(c * wall, wall), :] = high
-                load[1, pl.ds(c * wall, wall), :] = low
-
-            def scatter(t, carry):
-                high, low = parts(cross[t].reshape(STEP * BAND, markers))
-                value = dot(high, load[0], 1) + dot(low, load[0], 1) + dot(high, load[1], 1)
-                for c in range(3):
-                    force[c, pl.ds(x0 + t * STEP, STEP), pl.ds(zb, BAND), :] += value[
-                        :, c * wall : (c + 1) * wall
-                    ].reshape(STEP, BAND, wall)
-                return carry
-
-            lax.fori_loop(0, BOX // STEP, scatter, 0)
+                loads.append((target - sampled[c : c + 1]) * weight_z)
+            load = parts(jnp.concatenate(loads))
+            value = pair(load, (cross[0], cross[1]), 1).reshape(3, BAND, BOX * BAND)
+            inside = (lane >= y0) & (lane < y0 + BOX)
+            for i in range(BOX):
+                q, r = i // many, i % many
+                piece = value[:, :, q * wall : (q + 1) * wall]
+                piece = pltpu.roll(piece, lax.rem(wall + y0 - r * BAND, wall), 2)
+                force[:, x0 + i, pl.ds(zb, BAND), :] += jnp.where(inside, piece, 0.0)
 
         return carry
 
     lax.fori_loop(0, ids.shape[0], one_slot, 0)
 
 
-def spread_forces(extended, slot_ids, starts, cells, fracs, moving, turning):
+def spread_forces(nx, nz, extended, slot_ids, corners, cells, fracs, moving, turning):
     _, slots, markers = cells.shape
-    wall = extended.shape[3]
     scalar = pl.BlockSpec(memory_space=pltpu.SMEM)
     vector = pl.BlockSpec(memory_space=pltpu.VMEM)
     return pl.pallas_call(
-        marker_kernel,
+        functools.partial(marker_kernel, nx, nz),
         out_shape=jax.ShapeDtypeStruct(extended.shape, jnp.float32),
         in_specs=[scalar] * 4 + [vector] * 3,
         out_specs=vector,
         scratch_shapes=[
             pltpu.VMEM((4, 3, slots, markers), jnp.float32),
-            pltpu.VMEM((BOX // STEP, STEP, BAND, markers), jnp.float32),
-            pltpu.VMEM((wall, markers), jnp.float32),
-            pltpu.VMEM((2, wall, markers), jnp.bfloat16),
-            pltpu.VMEM((2, 3 * wall, markers), jnp.bfloat16),
+            pltpu.VMEM((2, BOX * BAND, markers), jnp.bfloat16),
         ],
+        compiler_params=pltpu.CompilerParams(vmem_limit_bytes=24 << 20),
         name="markers",
-    )(slot_ids, starts, moving, turning, cells, fracs, extended)
+    )(slot_ids, corners, moving, turning, cells, fracs, extended)
 
 
 def dot3(high, low, other_high, other_low):
@@ -584,7 +586,9 @@
             dma((2, 3)), dma((2, 3)), dma((2, 3)), dma((2, 3)), dma((4,)), dma((4,)),
             dma((nz,)), dma((nz,)), dma((nx,)), dma((nx,)),
         ],
-        compiler_params=pltpu.CompilerParams(collective_id=1, has_side_effects=True),
+        compiler_params=pltpu.CompilerParams(
+            collective_id=1, has_side_effects=True, vmem_limit_bytes=28 << 20
+        ),
         name="spectrum",
     )(force, field, jnp.asarray(table_z), jnp.asarray(table_x))
 
@@ -593,20 +597,13 @@
     nx, nz, flow_state, slot_ids, corners, marker_cells, marker_frac, particle_velocity,
     particle_spin,
 ):
-    tile_x = flow_state.shape[1]
-    tile_z = flow_state.shape[2]
     extended = predict(flow_state, nx, nz)
-    starts = jnp.stack(
-        [
-            (corners[0] - lax.axis_index("gx") * tile_x + HALF) % (tile_x * nx),
-            corners[1],
-            (corners[2] - lax.axis_index("gz") * tile_z + SIDE) % (tile_z * nz),
-        ]
-    )
     force = spread_forces(
+        nx,
+        nz,
         extended,
         slot_ids,
-        starts,
+        corners,
         marker_cells,
         marker_frac,
         particle_velocity,

time: 135 us -> 98.1 us (0.73)
  Pallas kernels: 130 us -> 94 us
  other arithmetic: 1.39 us -> 0 us
    pallas_call x1, Pallas kernels: 65.8 us -> 47.7 us  [spectrum(): pl.pallas_call(functools.partial(spectrum_kernel, nx, nz, 1.0 / math.sqrt...]
    pallas_call x1, Pallas kernels: 27.1 us -> 12.4 us  [spread_forces(): pl.pallas_call(functools.partial(marker_kernel, nx, nz), out_shape=jax.Sh...]
    pallas_call x1, Pallas kernels: 36.8 us -> 33.9 us  [predict(): pl.pallas_call(functools.partial(front_kernel, nx, nz), out_shape=jax.Sha...]
    unnamed x2 -> x20, local copies, waits for them, and re-layouts: 3.93 us -> 2.93 us
where the time goes in v2:
time: 98.1 us; the launch traced here: 97.7 us
  Pallas kernels  94 us (96%)
  local copies, waits for them, and re-layouts  2.93 us (3%)
    pallas_call x1, Pallas kernels, spectrum(): pl.pallas_call(functools.partial(spectrum_kernel, nx, nz, 1.0 / math.sqrt...  47.7 us
    pallas_call x1, Pallas kernels, predict(): pl.pallas_call(functools.partial(front_kernel, nx, nz), out_shape=jax.Sha...  33.9 us
    pallas_call x1, Pallas kernels, spread_forces(): pl.pallas_call(functools.partial(marker_kernel, nx, nz), out_shape=jax.Sh...  12.4 us
    unnamed x20, local copies, waits for them, and re-layouts  2.93 us

profile of v2, /device:TPU:1, one launch (start us, length us, event | category | flops | bytes accessed | tf_op | source)
XLA Modules:
  0.0 97.7 jit_solution(7485330972569111620)
XLA Ops:
  0.6 0.0 copy-start.1
  0.6 1.2 %copy-done.1 = f32[4,16,32,128]{3,2,1,0:T(8,128)S(1)} copy-done((f32[4,16,32,128]{3,2,1,0:T(8,128)S(1)}, f32[4,16,32,128]{3,2,1,0:T(8,128)}, u32[]{:S(2)}) %copy-start.1) | copy-done | bytes 1048600
  1.9 0.0 copy-start.3
  1.9 0.0 copy-start.4
  1.9 0.0 copy-start.5
  1.9 0.0 copy-start.6
  1.9 0.0 copy-start.7
  1.9 0.0 copy-start.8
  1.9 33.9 %front.1.field = f32[3,40,64,128]{3,2,1,0:T(8,128)S(1)} custom-call(f32[4,16,32,128]{3,2,1,0:T(8,128)S(1)} %copy-done.1), custom_call_target="tpu_custom_call" | custom-call | tf_op jit(solution)/shard_map/front/pallas_call | solution.py:167
  35.8 0.0 copy-done.3
  35.8 0.0 copy-done.4
  35.8 0.0 copy-done.5
  35.8 0.0 copy-done.6
  35.8 0.0 copy-done.7
  35.8 0.0 copy-done.8
  35.8 0.0 copy-start
  35.8 0.0 copy-start.2
  35.9 12.4 %markers.1.force = f32[3,40,64,128]{3,2,1,0:T(8,128)S(1)} custom-call(s32[8]{0:T(128)S(1)} %copy-done.8, s32[3,8]{1,0:T(4,128)S(1)} %copy-done.7, f32[3,1024]{1,0:T(4,128)S(1)} %copy-done.5, f32[3,1024]{1,0:T(4,128)S(1)} %copy-done.6, s32[3,8,512]{2,1,0:T(8,128)S(1)} %copy-done.3, f32[3,8,512]{2,1,0:T(8,128)S(1)} %copy-done.4, f32[3,40,64,128]{3,2,1,0:T(8,128)S(1)} %front.1.field), custom_call_target="tpu_custom_call" | custom-call | tf_op jit(solution)/shard_map/markers/pallas_call | solution.py:289
  48.3 0.0 copy-done
  48.3 0.0 copy-done.2
  48.3 47.7 %spectrum.1 = (f32[3,16,32,128]{3,2,1,0:T(8,128)S(1)}, f32[2,16,8,512]{3,2,1,0:T(8,128)S(1)}) custom-call(f32[3,40,64,128]{3,2,1,0:T(8,128)S(1)} %markers.1.force, f32[3,40,64,128]{3,2,1,0:T(8,128)S(1)} %front.1.field, bf16[2,512,256]{2,1,0:T(8,128)(2,1)S(1)} %copy-done.2, bf16[2,4,512,256]{3,2,1,0:T(8,128)(2,1)S(1)} %copy-done), custom_call_target="tpu_custom_call" | custom-call | tf_op jit(solution)/shard_map/spectrum/pallas_call | solution.py:567
  96.0 0.9 copy.13
  96.9 0.8 copy.14
Async XLA Ops:
  0.6 1.2 %copy-start.1 = (f32[4,16,32,128]{3,2,1,0:T(8,128)S(1)}, f32[4,16,32,128]{3,2,1,0:T(8,128)}, u32[]{:S(2)}) copy-start(f32[4,16,32,128]{3,2,1,0:T(8,128)} %flow.1) | copy-start | bytes 3145732
  1.9 33.9 %copy-start.3 = (s32[3,8,512]{2,1,0:T(8,128)S(1)}, s32[3,8,512]{2,1,0:T(8,128)}, u32[]{:S(2)}) copy-start(s32[3,8,512]{2,1,0:T(8,128)} %cells.1) | copy-start | bytes 147460
  1.9 33.9 %copy-start.4 = (f32[3,8,512]{2,1,0:T(8,128)S(1)}, f32[3,8,512]{2,1,0:T(8,128)}, u32[]{:S(2)}) copy-start(f32[3,8,512]{2,1,0:T(8,128)} %fracs.1) | copy-start | bytes 147460
  1.9 33.9 %copy-start.5 = (f32[3,1024]{1,0:T(4,128)S(1)}, f32[3,1024]{1,0:T(4,128)}, u32[]{:S(2)}) copy-start(f32[3,1024]{1,0:T(4,128)} %moving.1) | copy-start | bytes 36868
  1.9 33.9 %copy-start.6 = (f32[3,1024]{1,0:T(4,128)S(1)}, f32[3,1024]{1,0:T(4,128)}, u32[]{:S(2)}) copy-start(f32[3,1024]{1,0:T(4,128)} %turning.1) | copy-start | bytes 36868
  1.9 33.9 %copy-start.7 = (s32[3,8]{1,0:T(4,128)S(1)}, s32[3,8]{1,0:T(4,128)}, u32[]{:S(2)}) copy-start(s32[3,8]{1,0:T(4,128)} %corners.1) | copy-start | bytes 292
  1.9 33.9 %copy-start.8 = (s32[8]{0:T(128)S(1)}, s32[8]{0:T(128)}, u32[]{:S(2)}) copy-start(s32[8]{0:T(128)} %ids.1) | copy-start | bytes 100
  35.8 12.5 %copy-start = (bf16[2,4,512,256]{3,2,1,0:T(8,128)(2,1)S(1)}, bf16[2,4,512,256]{3,2,1,0:T(8,128)(2,1)}, u32[]{:S(2)}) copy-start(bf16[2,4,512,256]{3,2,1,0:T(8,128)(2,1)} %constant.5.clone.table_x) | copy-start | bytes 6291460
  35.8 12.5 %copy-start.2 = (bf16[2,512,256]{2,1,0:T(8,128)(2,1)S(1)}, bf16[2,512,256]{2,1,0:T(8,128)(2,1)}, u32[]{:S(2)}) copy-start(bf16[2,512,256]{2,1,0:T(8,128)(2,1)} %constant.4.clone.table_z) | copy-start | bytes 1572868

commit v3 on v2

--- a/solution.py
+++ b/solution.py
@@ -43,15 +43,20 @@
 
 
 def front_kernel(
-    nx, nz, flow, field, edge_x, edge_z_out, edge_z,
-    e_send, e_recv, x_send, x_recv, z_send, z_recv,
+    nx, nz, flow_in, field, flow, edge_x, edge_z_out, edge_z,
+    f_sem, e_send, e_recv, x_send, x_recv, z_send, z_recv,
 ):
     _, wide, tall, wall = flow.shape
     left, right, below, above = around(nx, nz)
     barrier = pltpu.get_barrier_semaphore()
     for near in (left, right, below, above):
         pl.semaphore_signal(barrier, inc=1, device_id=near, device_id_type=MESH)
+    loads = [pltpu.make_async_copy(flow_in.at[c], flow.at[c], f_sem.at[c]) for c in range(4)]
+    for load in loads:
+        load.start()
     pl.semaphore_wait(barrier, 4)
+    for load in loads:
+        load.wait()
     edge_z_out[0] = flow[:, :, 0, :]
     edge_z_out[1] = flow[:, :, tall - 1, :]
     edges = [
@@ -169,19 +174,21 @@
         out_shape=jax.ShapeDtypeStruct(
             (3, wide + 2 * HALF, tall + 2 * SIDE, wall), jnp.float32
         ),
-        in_specs=[pl.BlockSpec(memory_space=pltpu.VMEM)],
+        in_specs=[pl.BlockSpec(memory_space=pltpu.HBM)],
         out_specs=pl.BlockSpec(memory_space=pltpu.VMEM),
         scratch_shapes=[
+            pltpu.VMEM(flow.shape, jnp.float32),
             pltpu.VMEM((2, 4, tall, wall), jnp.float32),
             pltpu.VMEM((2, 4, wide, wall), jnp.float32),
             pltpu.VMEM((2, 4, wide, wall), jnp.float32),
-            dma((4,)), dma((4,)), dma((2, 3)), dma((2, 3)), dma((2, 3, 3)), dma((2, 3, 3)),
+            dma((4,)), dma((4,)), dma((4,)), dma((2, 3)), dma((2, 3)), dma((2, 3, 3)),
+            dma((2, 3, 3)),
         ],
         compiler_params=pltpu.CompilerParams(
             collective_id=0, has_side_effects=True, vmem_limit_bytes=12 << 20
         ),
         name="front",
-    )(flow)
+    )(pltpu.with_memory_space_constraint(flow, pltpu.HBM))
 
 
 def parts(value):
@@ -300,10 +307,6 @@
     )(slot_ids, corners, moving, turning, cells, fracs, extended)
 
 
-def dot3(high, low, other_high, other_low):
-    return dot(high, other_high, 0) + dot(low, other_high, 0) + dot(high, other_low, 0)
-
-
 def exchanged(rows, lane_bits):
     lane = lax.broadcasted_iota(jnp.int32, rows[0].shape, rows[0].ndim - 1)
     axis = rows[0].ndim - 1
@@ -321,15 +324,13 @@
 
 
 def spectrum_kernel(
-    nx, nz, scale, force, field, table_z, table_x, velocity, source,
-    z_got, x_out, x_got, edge_u, edge_w, edge_w_out, cut, planes, modes, rows,
+    nx, nz, force, field, table_z, velocity, rows,
+    z_got, x_out, x_got, u_out, u_got, row_out, row_got, row_sum, rim_out, rim_got, edge_u,
+    edge_w, cut, planes, modes,
     z_send, z_recv, x_send, x_recv, e_send, e_recv, c_send, c_recv, m_send, m_recv,
 ):
     gx, gz = lax.axis_index("gx"), lax.axis_index("gz")
-    below = (gx, lax.rem(gz + nz - 1, nz))
-    above = (gx, lax.rem(gz + 1, nz))
-    left = (lax.rem(gx + nx - 1, nx), gz)
-    right = (lax.rem(gx + 1, nx), gz)
+    left, right, below, above = around(nx, nz)
     barrier = pltpu.get_barrier_semaphore()
 
     def greet_z(d, carry):
@@ -344,82 +345,125 @@
         )
         return carry
 
+    lax.fori_loop(1, nx, greet_x, 0)
     lax.fori_loop(1, nz, greet_z, 0)
-    lax.fori_loop(1, nx, greet_x, 0)
+    wide, tall = velocity.shape[1], velocity.shape[2]
+    row_out[0] = force[2, :, SIDE, :]
+    row_out[1] = force[2, :, SIDE + tall - 1, :]
     pl.semaphore_wait(barrier, nx + nz - 2)
 
-    wide, tall = velocity.shape[1], velocity.shape[2]
     order = (0, 2, 1)
-    z_copies, x_copies = {}, {}
-    for c in order:
+    own = pl.ds(HALF, wide)
+    pieces = (pl.ds(0, HALF), pl.ds(HALF + wide, HALF), own)
+
+    def fold_z(c, piece):
+        columns = pieces[piece]
         down = remote(
-            force.at[c, :, pl.ds(0, SIDE), :], z_got.at[1, c], (z_send, z_recv), (1, c), below
+            force.at[c, columns, pl.ds(0, SIDE), :],
+            z_got.at[1, c, columns],
+            (z_send, z_recv), (1, c, piece), below,
         )
         up = remote(
-            force.at[c, :, pl.ds(SIDE + tall, SIDE), :],
-            z_got.at[0, c],
-            (z_send, z_recv),
-            (0, c),
-            above,
+            force.at[c, columns, pl.ds(SIDE + tall, SIDE), :],
+            z_got.at[0, c, columns],
+            (z_send, z_recv), (0, c, piece), above,
         )
         down.start()
         up.start()
-        z_copies[c] = (down, up)
+        return [down, up]
+
+    rims, inner = {}, {}
     for c in order:
-        for copy in z_copies[c]:
+        rims[c] = fold_z(c, 0) + fold_z(c, 1)
+        if c == 2:
+            lines = [
+                remote(row_out.at[0], row_got.at[1], (e_send, e_recv), 0, below),
+                remote(row_out.at[1], row_got.at[0], (e_send, e_recv), 1, above),
+            ]
+            for copy in lines:
+                copy.start()
+    for c in order:
+        inner[c] = fold_z(c, 2)
+    x_copies = {}
+    for c in order:
+        for copy in rims[c]:
             copy.wait_recv()
         for part in range(2):
-            inner = pl.ds(part * SIDE, SIDE)
-            outer = pl.ds(SIDE + part * SIDE, SIDE)
-            x_out[0, c, :, inner, :] = (
-                force[c, pl.ds(0, HALF), outer, :] + z_got[part, c, pl.ds(0, HALF)]
-            )
-            x_out[1, c, :, inner, :] = (
-                force[c, pl.ds(HALF + wide, HALF), outer, :]
-                + z_got[part, c, pl.ds(HALF + wide, HALF)]
-            )
+            inside = pl.ds(part * SIDE, SIDE)
+            outside = pl.ds(SIDE + part * SIDE, SIDE)
+            for side in range(2):
+                x_out[side, c, :, inside, :] = (
+                    force[c, pieces[side], outside, :] + z_got[part, c, pieces[side]]
+                )
         back = remote(x_out.at[0, c], x_got.at[1, c], (x_send, x_recv), (1, c), left)
         ahead = remote(x_out.at[1, c], x_got.at[0, c], (x_send, x_recv), (0, c), right)
         back.start()
         ahead.start()
-        x_copies[c] = (back, ahead)
+        x_copies[c] = [back, ahead]
+        if c == 2:
+            for copy in lines:
+                copy.wait_recv()
+            row_sum[0] = force[2, :, SIDE - 1, :] + row_got[0]
+            row_sum[1] = force[2, :, SIDE + tall, :] + row_got[1]
+            rim_out[0] = row_sum[:, pl.ds(0, HALF), :]
+            rim_out[1] = row_sum[:, pl.ds(HALF + wide, HALF), :]
+            ends = [
+                remote(rim_out.at[0], rim_got.at[1], (e_send, e_recv), 2, left),
+                remote(rim_out.at[1], rim_got.at[0], (e_send, e_recv), 3, right),
+            ]
+            for copy in ends:
+                copy.start()
+        if c == 0:
+            for copy in inner[0]:
+                copy.wait_recv()
+            for part in range(2):
+                inside = pl.ds(part * SIDE, SIDE)
+                outside = pl.ds(SIDE + part * SIDE, SIDE)
+                u_out[0, inside, :] = force[0, HALF, outside, :] + z_got[part, 0, HALF]
+                u_out[1, inside, :] = (
+                    force[0, HALF + wide - 1, outside, :] + z_got[part, 0, HALF + wide - 1]
+                )
+            layers = [
+                remote(u_out.at[0], u_got.at[1], (e_send, e_recv), 4, left),
+                remote(u_out.at[1], u_got.at[0], (e_send, e_recv), 5, right),
+            ]
+            for copy in layers:
+                copy.start()
+    for c in order:
+        if c != 0:
+            for copy in inner[c]:
+                copy.wait_recv()
         for part in range(2):
-            inner = pl.ds(part * SIDE, SIDE)
-            outer = pl.ds(SIDE + part * SIDE, SIDE)
-            velocity[c, :, inner, :] = (
-                field[c, pl.ds(HALF, wide), outer, :]
-                + force[c, pl.ds(HALF, wide), outer, :]
-                + z_got[part, c, pl.ds(HALF, wide)]
+            inside = pl.ds(part * SIDE, SIDE)
+            outside = pl.ds(SIDE + part * SIDE, SIDE)
+            velocity[c, :, inside, :] = (
+                field[c, own, outside, :] + force[c, own, outside, :] + z_got[part, c, own]
             )
-    edges = []
     for c in order:
         for copy in x_copies[c]:
             copy.wait_recv()
         velocity[c, pl.ds(0, HALF)] += x_got[0, c]
         velocity[c, pl.ds(wide - HALF, HALF)] += x_got[1, c]
         if c == 0:
-            edges += [
-                remote(velocity.at[0, 0], edge_u.at[1], (e_send, e_recv), 0, left),
-                remote(velocity.at[0, wide - 1], edge_u.at[0], (e_send, e_recv), 1, right),
-            ]
+            for copy in layers:
+                copy.wait_recv()
+            body = pl.ds(SIDE, tall)
+            edge_u[0] = field[0, HALF - 1, body, :] + x_out[0, 0, HALF - 1] + u_got[0]
+            edge_u[1] = field[0, HALF + wide, body, :] + x_out[1, 0, 0] + u_got[1]
         if c == 2:
-            edge_w_out[0] = velocity[2, :, 0, :]
-            edge_w_out[1] = velocity[2, :, tall - 1, :]
-            edges += [
-                remote(edge_w_out.at[0], edge_w.at[1], (e_send, e_recv), 2, below),
-                remote(edge_w_out.at[1], edge_w.at[0], (e_send, e_recv), 3, above),
-            ]
-        if c != 1:
-            edges[-2].start()
-            edges[-1].start()
+            for copy in ends:
+                copy.wait_recv()
+            edge_w[0] = field[2, own, SIDE - 1, :] + row_sum[0, own, :]
+            edge_w[1] = field[2, own, SIDE + tall, :] + row_sum[1, own, :]
+            edge_w[:, pl.ds(0, HALF), :] += rim_got[0]
+            edge_w[:, pl.ds(wide - HALF, HALF), :] += rim_got[1]
+    edges = lines + ends + layers
     wall = velocity.shape[3]
     lane = lax.broadcasted_iota(jnp.int32, (1, 1, wall), 2)
     normal = velocity[1]
     upper = jnp.where(lane == wall - 1, 0.0, pltpu.roll(normal, wall - 1, 2))
     lower = jnp.where(lane == 0, 0.0, pltpu.roll(normal, 1, 2))
     divergence = upper - lower
-    for copy in edges:
-        copy.wait_recv()
     stream = velocity[0]
     divergence += jnp.concatenate([stream[1:], edge_u[1:2]], axis=0) - jnp.concatenate(
         [edge_u[0:1], stream[:-1]], axis=0
@@ -481,10 +525,19 @@
     planes[gz] = cut[gz]
     lax.fori_loop(1, nz, wait_recv(cut_from), 0)
     high, low = parts(planes[...].reshape(nz * tall, 2 * 128))
-    modes[...] = dot3(table_z[0], table_z[1], high, low).reshape(modes.shape)
-
-    def mode_copy(d):
-        to = lax.rem(gx + d, nx)
+    modes[...] = pair((table_z[0], table_z[1]), (high, low), 0).reshape(modes.shape)
+
+    deep = nx // 8
+    deep_at, along_at = lax.div(gx, 8), lax.rem(gx, 8)
+
+    def partner(t):
+        k, j = lax.div(t, deep), lax.rem(t, deep)
+        odd = lax.rem(k, 2)
+        step = 4 - odd + lax.div(k, 2) * (1 - 2 * odd)
+        return lax.rem(deep_at + j + 1, deep) * 8 + lax.rem(along_at + step, 8)
+
+    def mode_copy(t):
+        to = partner(t)
         return pltpu.make_async_remote_copy(
             src_ref=modes.at[:, to],
             dst_ref=rows.at[gx],
@@ -494,8 +547,8 @@
             device_id_type=MESH,
         )
 
-    def mode_from(d):
-        origin = lax.rem(gx + d, nx)
+    def mode_from(t):
+        origin = partner(t)
         return pltpu.make_async_remote_copy(
             src_ref=modes.at[:, origin],
             dst_ref=rows.at[origin],
@@ -505,11 +558,23 @@
             device_id_type=MESH,
         )
 
-    lax.fori_loop(1, nx, start(mode_copy), 0)
+    lax.fori_loop(0, nx - 1, start(mode_copy), 0)
     rows[gx] = modes[:, gx]
-    lax.fori_loop(1, nx, wait_recv(mode_from), 0)
+    lax.fori_loop(0, nx - 1, wait_recv(mode_from), 0)
+    for c in order:
+        for copy in rims[c] + inner[c] + x_copies[c]:
+            copy.wait_send()
+    for copy in edges:
+        copy.wait_send()
+    lax.fori_loop(1, nz, wait_send(cut_copy), 0)
+    lax.fori_loop(0, nx - 1, wait_send(mode_copy), 0)
+
+
+def finish_kernel(scale, velocity_in, rows, table_x, velocity, source, held, sems):
+    through = pltpu.make_async_copy(velocity_in, velocity, sems.at[0])
+    through.start()
     columns = []
-    for h in range(nx // 16):
+    for h in range(rows.shape[0] // 16):
         for half in range(2):
             blocks = exchanged(
                 [rows[h * 16 + b, :, :, half * 128 : half * 128 + 128] for b in range(16)],
@@ -520,20 +585,21 @@
             )
     high, low = parts(jnp.concatenate(columns, axis=1))
     lines = high.shape[0] // 2
+    copies = [through]
     for q in range(table_x.shape[1]):
-        value = dot3(high, low, table_x[0, q], table_x[1, q])
+        value = pair((high, low), (table_x[0, q], table_x[1, q]), 0)
         real = value[:lines, :128] + value[lines:, 128:]
         imag = value[lines:, :128] - value[:lines, 128:]
         out = pl.ds(q * 128, 128)
-        source[0, :, :, out] = (real * scale).reshape(source.shape[1], source.shape[2], 128)
-        source[1, :, :, out] = (imag * scale).reshape(source.shape[1], source.shape[2], 128)
-    for c in order:
-        for copy in z_copies[c] + x_copies[c]:
-            copy.wait_send()
-    for copy in edges:
-        copy.wait_send()
-    lax.fori_loop(1, nz, wait_send(cut_copy), 0)
-    lax.fori_loop(1, nx, wait_send(mode_copy), 0)
+        held[0, :, :, out] = (real * scale).reshape(held.shape[1], held.shape[2], 128)
+        held[1, :, :, out] = (imag * scale).reshape(held.shape[1], held.shape[2], 128)
+        copy = pltpu.make_async_copy(
+            held.at[:, :, :, out], source.at[:, :, :, out], sems.at[1 + q]
+        )
+        copy.start()
+        copies.append(copy)
+    for copy in copies:
+        copy.wait()
 
 
 def split_table(table):
@@ -564,33 +630,55 @@
     dma = pltpu.SemaphoreType.DMA
     each = wall // nz
     deep = field.shape[1]
-    return pl.pallas_call(
-        functools.partial(spectrum_kernel, nx, nz, 1.0 / math.sqrt(length_x * length_z)),
+    modes = length_z // nx
+    velocity, rows = pl.pallas_call(
+        functools.partial(spectrum_kernel, nx, nz),
         out_shape=(
             jax.ShapeDtypeStruct(tile, jnp.float32),
-            jax.ShapeDtypeStruct((2, each, length_z // nx, length_x), jnp.float32),
+            jax.ShapeDtypeStruct((nx, 2, modes, wide * each), jnp.float32),
         ),
-        in_specs=[vector] * 4,
+        in_specs=[vector] * 3,
         out_specs=(vector, vector),
         scratch_shapes=[
             pltpu.VMEM((2, 3, deep, SIDE, wall), jnp.float32),
             pltpu.VMEM((2, 3, HALF, tall, wall), jnp.float32),
             pltpu.VMEM((2, 3, HALF, tall, wall), jnp.float32),
             pltpu.VMEM((2, tall, wall), jnp.float32),
-            pltpu.VMEM((2, wide, wall), jnp.float32),
+            pltpu.VMEM((2, tall, wall), jnp.float32),
+            pltpu.VMEM((2, deep, wall), jnp.float32),
+            pltpu.VMEM((2, deep, wall), jnp.float32),
+            pltpu.VMEM((2, deep, wall), jnp.float32),
+            pltpu.VMEM((2, 2, HALF, wall), jnp.float32),
+            pltpu.VMEM((2, 2, HALF, wall), jnp.float32),
+            pltpu.VMEM((2, tall, wall), jnp.float32),
             pltpu.VMEM((2, wide, wall), jnp.float32),
             pltpu.VMEM((nz, tall, wide * each), jnp.float32),
             pltpu.VMEM((nz, tall, wide * each), jnp.float32),
-            pltpu.VMEM((2, nx, length_z // nx, wide * each), jnp.float32),
-            pltpu.VMEM((nx, 2, length_z // nx, wide * each), jnp.float32),
-            dma((2, 3)), dma((2, 3)), dma((2, 3)), dma((2, 3)), dma((4,)), dma((4,)),
+            pltpu.VMEM((2, nx, modes, wide * each), jnp.float32),
+            dma((2, 3, 3)), dma((2, 3, 3)), dma((2, 3)), dma((2, 3)), dma((6,)), dma((6,)),
             dma((nz,)), dma((nz,)), dma((nx,)), dma((nx,)),
         ],
         compiler_params=pltpu.CompilerParams(
             collective_id=1, has_side_effects=True, vmem_limit_bytes=28 << 20
         ),
         name="spectrum",
-    )(force, field, jnp.asarray(table_z), jnp.asarray(table_x))
+    )(force, field, jnp.asarray(table_z))
+    shape = (2, each, modes, length_x)
+    return pl.pallas_call(
+        functools.partial(finish_kernel, 1.0 / math.sqrt(length_x * length_z)),
+        out_shape=(
+            jax.ShapeDtypeStruct(tile, jnp.float32),
+            jax.ShapeDtypeStruct(shape, jnp.float32),
+        ),
+        in_specs=[vector] * 3,
+        out_specs=(pl.BlockSpec(memory_space=pltpu.HBM), pl.BlockSpec(memory_space=pltpu.HBM)),
+        scratch_shapes=[
+            pltpu.VMEM(shape, jnp.float32),
+            dma((1 + length_x // 128,)),
+        ],
+        compiler_params=pltpu.CompilerParams(vmem_limit_bytes=16 << 20),
+        name="finish",
+    )(velocity, rows, jnp.asarray(table_x))
 
 
 def on_device(

time: 98.1 us -> 97.2 us (level)
  local copies, waits for them, and re-layouts: 2.93 us -> 0.04 us
  Pallas kernels: 94 us -> 96.3 us
    pallas_call x1 -> x2, Pallas kernels: 47.7 us -> 54.6 us  [the longest x1 52.4 us: spectrum(): pl.pallas_call(functools.partial(spectrum_kernel, nx, nz), out_shape=(jax...]
    pallas_call x1, Pallas kernels: 12.4 us -> 7.81 us  [spread_forces(): pl.pallas_call(functools.partial(marker_kernel, nx, nz), out_shape=jax.Sh...]
    unnamed x20 -> x16, local copies, waits for them, and re-layouts: 2.93 us -> 0.04 us
where the time goes in v3:
time: 97.2 us
  Pallas kernels  96.3 us (99%)
    pallas_call x1, Pallas kernels, spectrum(): pl.pallas_call(functools.partial(spectrum_kernel, nx, nz), out_shape=(jax...  52.4 us
    pallas_call x1, Pallas kernels, predict(): pl.pallas_call(functools.partial(front_kernel, nx, nz), out_shape=jax.Sha...  33.9 us
    pallas_call x1, Pallas kernels, spread_forces(): pl.pallas_call(functools.partial(marker_kernel, nx, nz), out_shape=jax.Sh...  7.81 us
    pallas_call x1, Pallas kernels, spectrum(): pl.pallas_call(functools.partial(finish_kernel, 1.0 / math.sqrt(length_x...  2.21 us

profile of v3, /device:TPU:1, one launch (start us, length us, event | category | flops | bytes accessed | tf_op | source)
XLA Modules:
  0.0 97.2 jit_solution(13104285028907742353)
XLA Ops:
  0.6 0.0 copy-start.5
  0.6 0.0 copy-start.4
  0.7 0.0 copy-start.3
  0.7 0.0 copy-start.2
  0.7 0.0 copy-start.6
  0.7 0.0 copy-start.7
  0.7 33.9 %front.1.field = f32[3,40,64,128]{3,2,1,0:T(8,128)S(1)} custom-call(f32[4,16,32,128]{3,2,1,0:T(8,128)} %flow_in.1), custom_call_target="tpu_custom_call" | custom-call | tf_op jit(solution)/shard_map/front/pallas_call | solution.py:172
  34.6 0.0 copy-done.5
  34.6 0.0 copy-done.4
  34.6 0.0 copy-done.3
  34.7 0.0 copy-done.2
  34.7 0.0 copy-done.6
  34.7 0.0 copy-done.7
  34.7 0.0 copy-start.1
  34.7 7.8 %markers.1.force = f32[3,40,64,128]{3,2,1,0:T(8,128)S(1)} custom-call(s32[8]{0:T(128)S(1)} %copy-done.7, s32[3,8]{1,0:T(4,128)S(1)} %copy-done.6, f32[3,1024]{1,0:T(4,128)S(1)} %copy-done.4, f32[3,1024]{1,0:T(4,128)S(1)} %copy-done.5, s32[3,8,512]{2,1,0:T(8,128)S(1)} %copy-done.2, f32[3,8,512]{2,1,0:T(8,128)S(1)} %copy-done.3, f32[3,40,64,128]{3,2,1,0:T(8,128)S(1)} %front.1.field), custom_call_target="tpu_custom_call" | custom-call | tf_op jit(solution)/shard_map/markers/pallas_call | solution.py:296
  42.5 0.0 copy-done.1
  42.5 0.0 copy-start
  42.5 52.4 %spectrum.1 = (f32[3,16,32,128]{3,2,1,0:T(8,128)S(1)}, f32[32,2,8,256]{3,2,1,0:T(8,128)S(1)}) custom-call(f32[3,40,64,128]{3,2,1,0:T(8,128)S(1)} %markers.1.force, f32[3,40,64,128]{3,2,1,0:T(8,128)S(1)} %front.1.field, bf16[2,512,256]{2,1,0:T(8,128)(2,1)S(1)} %copy-done.1), custom_call_target="tpu_custom_call" | custom-call | tf_op jit(solution)/shard_map/spectrum/pallas_call | solution.py:634
  94.9 0.0 copy-done
  94.9 2.2 %finish.1 = (f32[3,16,32,128]{3,2,1,0:T(8,128)}, f32[2,16,8,512]{3,2,1,0:T(8,128)}) custom-call(f32[3,16,32,128]{3,2,1,0:T(8,128)S(1)} %get-tuple-element.4.velocity_in, f32[32,2,8,256]{3,2,1,0:T(8,128)S(1)} %get-tuple-element.5.rows, bf16[2,4,512,256]{3,2,1,0:T(8,128)(2,1)S(1)} %copy-done), custom_call_target="tpu_custom_call" | custom-call | tf_op jit(solution)/shard_map/finish/pallas_call | solution.py:667
Async XLA Ops:
  0.6 34.0 %copy-start.5 = (f32[3,1024]{1,0:T(4,128)S(1)}, f32[3,1024]{1,0:T(4,128)}, u32[]{:S(2)}) copy-start(f32[3,1024]{1,0:T(4,128)} %turning.1) | copy-start | bytes 36868
  0.6 34.0 %copy-start.4 = (f32[3,1024]{1,0:T(4,128)S(1)}, f32[3,1024]{1,0:T(4,128)}, u32[]{:S(2)}) copy-start(f32[3,1024]{1,0:T(4,128)} %moving.1) | copy-start | bytes 36868
  0.7 34.0 %copy-start.3 = (f32[3,8,512]{2,1,0:T(8,128)S(1)}, f32[3,8,512]{2,1,0:T(8,128)}, u32[]{:S(2)}) copy-start(f32[3,8,512]{2,1,0:T(8,128)} %fracs.1) | copy-start | bytes 147460
  0.7 34.0 %copy-start.2 = (s32[3,8,512]{2,1,0:T(8,128)S(1)}, s32[3,8,512]{2,1,0:T(8,128)}, u32[]{:S(2)}) copy-start(s32[3,8,512]{2,1,0:T(8,128)} %cells.1) | copy-start | bytes 147460
  0.7 34.0 %copy-start.6 = (s32[3,8]{1,0:T(4,128)S(1)}, s32[3,8]{1,0:T(4,128)}, u32[]{:S(2)}) copy-start(s32[3,8]{1,0:T(4,128)} %corners.1) | copy-start | bytes 292
  0.7 34.0 %copy-start.7 = (s32[8]{0:T(128)S(1)}, s32[8]{0:T(128)}, u32[]{:S(2)}) copy-start(s32[8]{0:T(128)} %ids.1) | copy-start | bytes 100
  34.7 7.8 %copy-start.1 = (bf16[2,512,256]{2,1,0:T(8,128)(2,1)S(1)}, bf16[2,512,256]{2,1,0:T(8,128)(2,1)}, u32[]{:S(2)}) copy-start(bf16[2,512,256]{2,1,0:T(8,128)(2,1)} %constant.4.clone.table_z) | copy-start | bytes 1572868
  42.5 52.4 %copy-start = (bf16[2,4,512,256]{3,2,1,0:T(8,128)(2,1)S(1)}, bf16[2,4,512,256]{3,2,1,0:T(8,128)(2,1)}, u32[]{:S(2)}) copy-start(bf16[2,4,512,256]{3,2,1,0:T(8,128)(2,1)} %constant.5.clone.table_x) | copy-start | bytes 6291460

commit v4 on v3

--- a/solution.py
+++ b/solution.py
@@ -42,9 +42,49 @@
     )
 
 
+def parts(value):
+    high = value.astype(jnp.bfloat16)
+    return high, (value - high.astype(jnp.float32)).astype(jnp.bfloat16)
+
+
+def tap_weights(length, first, taps):
+    offset = lax.broadcasted_iota(jnp.int32, (length, first.shape[-1]), 0) - first
+    weight = jnp.where(offset == 3, taps[3], 0.0)
+    for t in (2, 1, 0):
+        weight = jnp.where(offset == t, taps[t], weight)
+    return weight
+
+
+def fill_taps(fracs, tap):
+    angle = fracs[...] * (0.5 * math.pi)
+    cosine, sine = jnp.cos(angle), jnp.sin(angle)
+    tap[0] = 0.25 * (1.0 - sine)
+    tap[1] = 0.25 * (1.0 + cosine)
+    tap[2] = 0.25 * (1.0 + sine)
+    tap[3] = 0.25 * (1.0 - cosine)
+
+
+def cross_weights(cells, fracs, tap, cross):
+    fill_taps(fracs, tap)
+    markers = fracs.shape[2]
+
+    def one_slot(s, carry):
+        cell = cells[:, pl.ds(s, 1), :].reshape(3, markers)
+        taps = [tap[t, :, pl.ds(s, 1), :].reshape(3, markers) for t in range(4)]
+        weight_x = tap_weights(BOX, cell[0:1] - 1, [w[0:1] for w in taps])
+        weight_y = tap_weights(BAND, cell[1:2] - 1, [w[1:2] for w in taps])
+        for i in range(BOX):
+            high, low = parts(weight_x[i : i + 1] * weight_y)
+            cross[s, 0, pl.ds(i * BAND, BAND), :] = high
+            cross[s, 1, pl.ds(i * BAND, BAND), :] = low
+        return carry
+
+    lax.fori_loop(0, cells.shape[1], one_slot, 0)
+
+
 def front_kernel(
-    nx, nz, flow_in, field, flow, edge_x, edge_z_out, edge_z,
-    f_sem, e_send, e_recv, x_send, x_recv, z_send, z_recv,
+    nx, nz, flow_in, cells, fracs, field, cross, tap, flow, edge_x, edge_z_out, edge_z,
+    f_sem, e_send, e_recv, x_send, x_recv, z_send, z_recv, r_send, r_recv,
 ):
     _, wide, tall, wall = flow.shape
     left, right, below, above = around(nx, nz)
@@ -108,6 +148,54 @@
         return carry
 
     lax.fori_loop(1, wide - 1, inside, 0)
+    rim = HALF - 1
+    half = SIDE // 2
+    spans = (
+        {0: (1, rim), 1: (0, 1), 2: (0, HALF), 3: (0, HALF)},
+        {0: (0, rim), 1: (rim, 1), 2: (0, HALF), 3: (0, HALF)},
+    )
+    lines = {0: (half, SIDE), 1: (half, SIDE), 2: (0, half), 3: (tall - half, half)}
+    x_copies, z_copies = {}, []
+
+    def send(c, piece):
+        for side in range(2):
+            first, count = spans[side][piece]
+            at, height = lines[piece]
+            source, target = ((HALF, HALF + wide), (wide, 0))[side]
+            rows = pl.ds(SIDE + at, height)
+            copy = remote(
+                field.at[c, pl.ds(source + first, count), rows],
+                field.at[c, pl.ds(target + first, count), rows],
+                (x_send, x_recv), (side, c, piece), (left, right)[side],
+            )
+            copy.start()
+            x_copies[c, piece, side] = copy
+
+    def forward(c, piece, side):
+        first, count = spans[side][piece]
+        columns = pl.ds((HALF + wide, 0)[side] + first, count)
+        at, height = lines[piece]
+        slot = min(piece, 2)
+        if piece != 3:
+            copy = remote(
+                field.at[c, columns, pl.ds(SIDE + at, half)],
+                field.at[c, columns, pl.ds(SIDE + tall + at, half)],
+                (r_send, r_recv), (0, c, side, slot), below,
+            )
+            copy.start()
+            z_copies.append(copy)
+        if piece != 2:
+            start = at + height - half
+            copy = remote(
+                field.at[c, columns, pl.ds(SIDE + start, half)],
+                field.at[c, columns, pl.ds(SIDE + start - tall, half)],
+                (r_send, r_recv), (1, c, side, slot), above,
+            )
+            copy.start()
+            z_copies.append(copy)
+
+    for c in range(3):
+        send(c, 0)
     for copy in edges:
         copy.wait_recv()
     layer(0, [edge_x[0, c] for c in range(4)], [flow[c, 1] for c in range(4)])
@@ -115,7 +203,6 @@
         wide - 1, [flow[c, wide - 2] for c in range(4)], [edge_x[1, c] for c in range(4)]
     )
     own = pl.ds(HALF, wide)
-    x_copies, z_copies = [], []
     for c in range(3):
         for side, z, sign in ((0, 0, 1.0), (1, tall - 1, -1.0)):
             move = carry_by * edge_z_out[side, 2]
@@ -123,85 +210,62 @@
             if c == 2:
                 add += sign * carry_by * edge_z[side, 3]
             field[c, own, SIDE + z, :] += add
-        inner = pl.ds(SIDE, tall)
-        back = remote(
-            field.at[c, pl.ds(HALF, HALF), inner],
-            field.at[c, pl.ds(HALF + wide, HALF), inner],
-            (x_send, x_recv), (0, c), left,
-        )
-        ahead = remote(
-            field.at[c, pl.ds(wide, HALF), inner],
-            field.at[c, pl.ds(0, HALF), inner],
-            (x_send, x_recv), (1, c), right,
-        )
-        back.start()
-        ahead.start()
-        x_copies.append((back, ahead))
-
-    def slabs(c, piece, columns):
+        for piece in (2, 3, 1):
+            send(c, piece)
+    for c in range(3):
         down = remote(
-            field.at[c, columns, pl.ds(SIDE, SIDE)],
-            field.at[c, columns, pl.ds(SIDE + tall, SIDE)],
-            (z_send, z_recv), (0, c, piece), below,
+            field.at[c, own, pl.ds(SIDE, SIDE)],
+            field.at[c, own, pl.ds(SIDE + tall, SIDE)],
+            (z_send, z_recv), (0, c), below,
         )
         up = remote(
-            field.at[c, columns, pl.ds(tall, SIDE)],
-            field.at[c, columns, pl.ds(0, SIDE)],
-            (z_send, z_recv), (1, c, piece), above,
+            field.at[c, own, pl.ds(tall, SIDE)],
+            field.at[c, own, pl.ds(0, SIDE)],
+            (z_send, z_recv), (1, c), above,
         )
         down.start()
         up.start()
         z_copies.extend((down, up))
-
-    for c in range(3):
-        slabs(c, 0, own)
-    for c in range(3):
-        x_copies[c][0].wait_recv()
-        slabs(c, 1, pl.ds(HALF + wide, HALF))
-        x_copies[c][1].wait_recv()
-        slabs(c, 2, pl.ds(0, HALF))
+    cross_weights(cells, fracs, tap, cross)
+    for c, piece in [(c, 0) for c in range(3)] + [(c, p) for c in range(3) for p in (2, 3, 1)]:
+        for side in range(2):
+            x_copies[c, piece, side].wait_recv()
+            forward(c, piece, side)
     for copy in z_copies:
         copy.wait_recv()
-    for copy in edges + z_copies + [copy for pair in x_copies for copy in pair]:
+    for copy in edges + z_copies + list(x_copies.values()):
         copy.wait_send()
 
 
-def predict(flow, nx, nz):
+def predict(flow, cells, fracs, nx, nz):
     _, wide, tall, wall = flow.shape
+    _, slots, markers = cells.shape
+    vector = pl.BlockSpec(memory_space=pltpu.VMEM)
     dma = pltpu.SemaphoreType.DMA
     return pl.pallas_call(
         functools.partial(front_kernel, nx, nz),
-        out_shape=jax.ShapeDtypeStruct(
-            (3, wide + 2 * HALF, tall + 2 * SIDE, wall), jnp.float32
+        out_shape=(
+            jax.ShapeDtypeStruct(
+                (3, wide + 2 * HALF, tall + 2 * SIDE, wall), jnp.float32
+            ),
+            jax.ShapeDtypeStruct((slots, 2, BOX * BAND, markers), jnp.bfloat16),
         ),
-        in_specs=[pl.BlockSpec(memory_space=pltpu.HBM)],
-        out_specs=pl.BlockSpec(memory_space=pltpu.VMEM),
+        in_specs=[pl.BlockSpec(memory_space=pltpu.HBM), vector, vector],
+        out_specs=(vector, vector),
         scratch_shapes=[
+            pltpu.VMEM((4,) + cells.shape, jnp.float32),
             pltpu.VMEM(flow.shape, jnp.float32),
             pltpu.VMEM((2, 4, tall, wall), jnp.float32),
             pltpu.VMEM((2, 4, wide, wall), jnp.float32),
             pltpu.VMEM((2, 4, wide, wall), jnp.float32),
-            dma((4,)), dma((4,)), dma((4,)), dma((2, 3)), dma((2, 3)), dma((2, 3, 3)),
-            dma((2, 3, 3)),
+            dma((4,)), dma((4,)), dma((4,)), dma((2, 3, 4)), dma((2, 3, 4)), dma((2, 3)),
+            dma((2, 3)), dma((2, 3, 2, 3)), dma((2, 3, 2, 3)),
         ],
         compiler_params=pltpu.CompilerParams(
             collective_id=0, has_side_effects=True, vmem_limit_bytes=12 << 20
         ),
         name="front",
-    )(pltpu.with_memory_space_constraint(flow, pltpu.HBM))
-
-
-def parts(value):
-    high = value.astype(jnp.bfloat16)
-    return high, (value - high.astype(jnp.float32)).astype(jnp.bfloat16)
-
-
-def tap_weights(length, first, taps):
-    offset = lax.broadcasted_iota(jnp.int32, (length, first.shape[-1]), 0) - first
-    weight = jnp.where(offset == 3, taps[3], 0.0)
-    for t in (2, 1, 0):
-        weight = jnp.where(offset == t, taps[t], weight)
-    return weight
+    )(pltpu.with_memory_space_constraint(flow, pltpu.HBM), cells, fracs)
 
 
 def dot(a, b, across):
@@ -217,16 +281,10 @@
 
 
 def marker_kernel(
-    nx, nz, ids, corners, moving, turning, cells, fracs, field, force, tap, cross
+    nx, nz, ids, corners, moving, turning, cells, fracs, field, cross, force, tap
 ):
     force[...] = jnp.zeros_like(force)
-    half_pi = 0.5 * math.pi
-    angle = fracs[...] * half_pi
-    cosine, sine = jnp.cos(angle), jnp.sin(angle)
-    tap[0] = 0.25 * (1.0 - sine)
-    tap[1] = 0.25 * (1.0 + cosine)
-    tap[2] = 0.25 * (1.0 + sine)
-    tap[3] = 0.25 * (1.0 - cosine)
+    fill_taps(fracs, tap)
     markers = fracs.shape[2]
     wall = field.shape[3]
     wide, tall = field.shape[1] - 2 * HALF, field.shape[2] - 2 * SIDE
@@ -247,16 +305,7 @@
             frac = fracs[:, pl.ds(s, 1), :].reshape(3, markers)
             taps = [tap[t, :, pl.ds(s, 1), :].reshape(3, markers) for t in range(4)]
 
-            def along(d):
-                return [w[d : d + 1] for w in taps]
-
-            weight_x = tap_weights(BOX, cell[0:1] - 1, along(0))
-            weight_y = tap_weights(BAND, cell[1:2] - 1, along(1))
-            weight_z = tap_weights(BAND, cell[2:3] - 1 + (z0 - zb), along(2))
-            for i in range(BOX):
-                high, low = parts(weight_x[i : i + 1] * weight_y)
-                cross[0, pl.ds(i * BAND, BAND), :] = high
-                cross[1, pl.ds(i * BAND, BAND), :] = low
+            weight_z = tap_weights(BAND, cell[2:3] - 1 + (z0 - zb), [w[2:3] for w in taps])
             columns = []
             for q in range(BOX // many):
                 packed = None
@@ -266,7 +315,7 @@
                     packed = piece if r == 0 else jnp.where(lane < r * BAND, packed, piece)
                 columns.append(packed.reshape(3 * BAND, wall))
             window = parts(jnp.concatenate(columns, axis=1))
-            value = pair(window, (cross[0], cross[1]), 0).reshape(3, BAND, markers)
+            value = pair(window, (cross[s, 0], cross[s, 1]), 0).reshape(3, BAND, markers)
             sampled = jnp.sum(value * weight_z[None], axis=1)
             lever = cell.astype(jnp.float32) + frac - float(HALF)
             spin = [turning[c, n] for c in range(3)]
@@ -276,7 +325,7 @@
                 target = moving[c, n] + (spin[a] * lever[b : b + 1] - spin[b] * lever[a : a + 1])
                 loads.append((target - sampled[c : c + 1]) * weight_z)
             load = parts(jnp.concatenate(loads))
-            value = pair(load, (cross[0], cross[1]), 1).reshape(3, BAND, BOX * BAND)
+            value = pair(load, (cross[s, 0], cross[s, 1]), 1).reshape(3, BAND, BOX * BAND)
             inside = (lane >= y0) & (lane < y0 + BOX)
             for i in range(BOX):
                 q, r = i // many, i % many
@@ -289,22 +338,21 @@
     lax.fori_loop(0, ids.shape[0], one_slot, 0)
 
 
-def spread_forces(nx, nz, extended, slot_ids, corners, cells, fracs, moving, turning):
+def spread_forces(nx, nz, extended, cross, slot_ids, corners, cells, fracs, moving, turning):
     _, slots, markers = cells.shape
     scalar = pl.BlockSpec(memory_space=pltpu.SMEM)
     vector = pl.BlockSpec(memory_space=pltpu.VMEM)
     return pl.pallas_call(
         functools.partial(marker_kernel, nx, nz),
         out_shape=jax.ShapeDtypeStruct(extended.shape, jnp.float32),
-        in_specs=[scalar] * 4 + [vector] * 3,
+        in_specs=[scalar] * 4 + [vector] * 4,
         out_specs=vector,
         scratch_shapes=[
             pltpu.VMEM((4, 3, slots, markers), jnp.float32),
-            pltpu.VMEM((2, BOX * BAND, markers), jnp.bfloat16),
         ],
-        compiler_params=pltpu.CompilerParams(vmem_limit_bytes=24 << 20),
+        compiler_params=pltpu.CompilerParams(vmem_limit_bytes=16 << 20),
         name="markers",
-    )(slot_ids, corners, moving, turning, cells, fracs, extended)
+    )(slot_ids, corners, moving, turning, cells, fracs, extended, cross)
 
 
 def exchanged(rows, lane_bits):
@@ -685,11 +733,12 @@
     nx, nz, flow_state, slot_ids, corners, marker_cells, marker_frac, particle_velocity,
     particle_spin,
 ):
-    extended = predict(flow_state, nx, nz)
+    extended, cross = predict(flow_state, marker_cells, marker_frac, nx, nz)
     force = spread_forces(
         nx,
         nz,
         extended,
+        cross,
         slot_ids,
         corners,
         marker_cells,

time: 97.2 us -> 99.6 us (1.025); the launches traced: 97.2 us -> 98.3 us
  local copies, waits for them, and re-layouts: 0.04 us -> 5.96 us
  Pallas kernels: 96.3 us -> 91.6 us
    pallas_call x1, Pallas kernels: 7.81 us -> 1.64 us  [spread_forces(): pl.pallas_call(functools.partial(marker_kernel, nx, nz), out_shape=jax.Sh...]
    unnamed x16 -> x20, local copies, waits for them, and re-layouts: 0.04 us -> 5.96 us
    pallas_call x1, Pallas kernels: 52.4 us -> 57.4 us  [spectrum(): pl.pallas_call(functools.partial(spectrum_kernel, nx, nz), out_shape=(jax...]
    pallas_call x1, Pallas kernels: 33.9 us -> 30.3 us  [predict(): pl.pallas_call(functools.partial(front_kernel, nx, nz), out_shape=(jax.Sh...]
where the time goes in v4:
time: 99.6 us; the launch traced here: 98.3 us
  Pallas kernels  91.6 us (92%)
  local copies, waits for them, and re-layouts  5.96 us (6%)
    pallas_call x1, Pallas kernels, spectrum(): pl.pallas_call(functools.partial(spectrum_kernel, nx, nz), out_shape=(jax...  57.4 us
    pallas_call x1, Pallas kernels, predict(): pl.pallas_call(functools.partial(front_kernel, nx, nz), out_shape=(jax.Sh...  30.3 us
    unnamed x20, local copies, waits for them, and re-layouts  5.96 us
    pallas_call x1, Pallas kernels, spectrum(): pl.pallas_call(functools.partial(finish_kernel, 1.0 / math.sqrt(length_x...  2.21 us

profile of v4, /device:TPU:1, one launch (start us, length us, event | category | flops | bytes accessed | tf_op | source)
XLA Modules:
  0.0 98.3 jit_solution(17737230435272816361)
XLA Ops:
  0.6 0.0 copy-start.2
  0.6 0.8 copy-done.2
  1.4 0.0 copy-start.4
  1.4 0.8 copy-done.4
  2.2 30.3 %front.1 = (f32[3,40,64,128]{3,2,1,0:T(8,128)S(1)}, bf16[8,2,768,512]{3,2,1,0:T(8,128)(2,1)S(1)}) custom-call(f32[4,16,32,128]{3,2,1,0:T(8,128)} %flow_in.1, s32[3,8,512]{2,1,0:T(8,128)S(1)} %copy-done.2, f32[3,8,512]{2,1,0:T(8,128)S(1)} %copy-done.4), custom_call_target="tpu_custom_call" | custom-call | tf_op jit(solution)/shard_map/front/pallas_call | solution.py:245
  32.6 0.0 copy-start.3
  32.6 0.8 copy-done.3
  33.4 0.0 copy-start.5
  33.4 0.8 copy-done.5
  34.2 0.0 copy-start.6
  34.2 0.7 copy-done.6
  34.9 0.0 copy-start.7
  34.9 0.7 copy-done.7
  35.6 0.0 copy-start.8
  35.6 0.7 copy-done.8
  36.3 0.0 copy-start.9
  36.3 0.7 copy-done.9
  36.9 0.0 copy-start.1
  36.9 1.6 %markers.1.force = f32[3,40,64,128]{3,2,1,0:T(8,128)S(1)} custom-call(s32[8]{0:T(128)S(1)} %copy-done.9, s32[3,8]{1,0:T(4,128)S(1)} %copy-done.8, f32[3,1024]{1,0:T(4,128)S(1)} %copy-done.6, f32[3,1024]{1,0:T(4,128)S(1)} %copy-done.7, s32[3,8,512]{2,1,0:T(8,128)S(1)} %copy-done.3, f32[3,8,512]{2,1,0:T(8,128)S(1)} %copy-done.5, ...), custom_call_target="tpu_custom_call" | custom-call | tf_op jit(solution)/shard_map/markers/pallas_call | solution.py:345
  38.6 0.0 copy-done.1
  38.6 0.0 copy-start
  38.6 57.4 %spectrum.1 = (f32[3,16,32,128]{3,2,1,0:T(8,128)S(1)}, f32[32,2,8,256]{3,2,1,0:T(8,128)S(1)}) custom-call(f32[3,40,64,128]{3,2,1,0:T(8,128)S(1)} %markers.1.force, f32[3,40,64,128]{3,2,1,0:T(8,128)S(1)} %get-tuple-element.6.field, bf16[2,512,256]{2,1,0:T(8,128)(2,1)S(1)} %copy-done.1), custom_call_target="tpu_custom_call" | custom-call | tf_op jit(solution)/shard_map/spectrum/pallas_call | solution.py:682
  96.0 0.0 copy-done
  96.1 2.2 %finish.1 = (f32[3,16,32,128]{3,2,1,0:T(8,128)}, f32[2,16,8,512]{3,2,1,0:T(8,128)}) custom-call(f32[3,16,32,128]{3,2,1,0:T(8,128)S(1)} %get-tuple-element.8.velocity_in, f32[32,2,8,256]{3,2,1,0:T(8,128)S(1)} %get-tuple-element.9.rows, bf16[2,4,512,256]{3,2,1,0:T(8,128)(2,1)S(1)} %copy-done), custom_call_target="tpu_custom_call" | custom-call | tf_op jit(solution)/shard_map/finish/pallas_call | solution.py:715
Async XLA Ops:
  0.6 0.8 copy-start.2
  1.4 0.8 copy-start.4
  32.6 0.8 copy-start.3
  33.4 0.8 copy-start.5
  34.2 0.7 copy-start.6
  34.9 0.7 copy-start.7
  35.6 0.7 copy-start.8
  36.3 0.7 copy-start.9
  36.9 1.7 %copy-start.1 = (bf16[2,512,256]{2,1,0:T(8,128)(2,1)S(1)}, bf16[2,512,256]{2,1,0:T(8,128)(2,1)}, u32[]{:S(2)}) copy-start(bf16[2,512,256]{2,1,0:T(8,128)(2,1)} %constant.4.clone.table_z) | copy-start | bytes 1572868
  38.6 57.5 %copy-start = (bf16[2,4,512,256]{3,2,1,0:T(8,128)(2,1)S(1)}, bf16[2,4,512,256]{3,2,1,0:T(8,128)(2,1)}, u32[]{:S(2)}) copy-start(bf16[2,4,512,256]{3,2,1,0:T(8,128)(2,1)} %constant.5.clone.table_x) | copy-start | bytes 6291460

commit v5 on v4

--- a/solution.py
+++ b/solution.py
@@ -83,7 +83,7 @@
 
 
 def front_kernel(
-    nx, nz, flow_in, cells, fracs, field, cross, tap, flow, edge_x, edge_z_out, edge_z,
+    nx, nz, flow_in, cells_in, fracs_in, field, cross, tap, cells, fracs, flow, edge_x, edge_z_out, edge_z,
     f_sem, e_send, e_recv, x_send, x_recv, z_send, z_recv, r_send, r_recv,
 ):
     _, wide, tall, wall = flow.shape
@@ -92,7 +92,11 @@
     for near in (left, right, below, above):
         pl.semaphore_signal(barrier, inc=1, device_id=near, device_id_type=MESH)
     loads = [pltpu.make_async_copy(flow_in.at[c], flow.at[c], f_sem.at[c]) for c in range(4)]
-    for load in loads:
+    lists = [
+        pltpu.make_async_copy(cells_in, cells, f_sem.at[4]),
+        pltpu.make_async_copy(fracs_in, fracs, f_sem.at[5]),
+    ]
+    for load in loads + lists:
         load.start()
     pl.semaphore_wait(barrier, 4)
     for load in loads:
@@ -226,6 +230,8 @@
         down.start()
         up.start()
         z_copies.extend((down, up))
+    for load in lists:
+        load.wait()
     cross_weights(cells, fracs, tap, cross)
     for c, piece in [(c, 0) for c in range(3)] + [(c, p) for c in range(3) for p in (2, 3, 1)]:
         for side in range(2):
@@ -249,23 +255,25 @@
                 (3, wide + 2 * HALF, tall + 2 * SIDE, wall), jnp.float32
             ),
             jax.ShapeDtypeStruct((slots, 2, BOX * BAND, markers), jnp.bfloat16),
+            jax.ShapeDtypeStruct((4,) + cells.shape, jnp.float32),
+            jax.ShapeDtypeStruct(cells.shape, jnp.int32),
+            jax.ShapeDtypeStruct(cells.shape, jnp.float32),
         ),
-        in_specs=[pl.BlockSpec(memory_space=pltpu.HBM), vector, vector],
-        out_specs=(vector, vector),
+        in_specs=[pl.BlockSpec(memory_space=pltpu.HBM)] * 3,
+        out_specs=(vector,) * 5,
         scratch_shapes=[
-            pltpu.VMEM((4,) + cells.shape, jnp.float32),
             pltpu.VMEM(flow.shape, jnp.float32),
             pltpu.VMEM((2, 4, tall, wall), jnp.float32),
             pltpu.VMEM((2, 4, wide, wall), jnp.float32),
             pltpu.VMEM((2, 4, wide, wall), jnp.float32),
-            dma((4,)), dma((4,)), dma((4,)), dma((2, 3, 4)), dma((2, 3, 4)), dma((2, 3)),
+            dma((6,)), dma((4,)), dma((4,)), dma((2, 3, 4)), dma((2, 3, 4)), dma((2, 3)),
             dma((2, 3)), dma((2, 3, 2, 3)), dma((2, 3, 2, 3)),
         ],
         compiler_params=pltpu.CompilerParams(
             collective_id=0, has_side_effects=True, vmem_limit_bytes=12 << 20
         ),
         name="front",
-    )(pltpu.with_memory_space_constraint(flow, pltpu.HBM), cells, fracs)
+    )(*(pltpu.with_memory_space_constraint(each, pltpu.HBM) for each in (flow, cells, fracs)))
 
 
 def dot(a, b, across):
@@ -281,10 +289,9 @@
 
 
 def marker_kernel(
-    nx, nz, ids, corners, moving, turning, cells, fracs, field, cross, force, tap
+    nx, nz, ids, corners, moving, turning, cells, fracs, tap, field, cross, force
 ):
     force[...] = jnp.zeros_like(force)
-    fill_taps(fracs, tap)
     markers = fracs.shape[2]
     wall = field.shape[3]
     wide, tall = field.shape[1] - 2 * HALF, field.shape[2] - 2 * SIDE
@@ -294,9 +301,9 @@
     lane = lax.broadcasted_iota(jnp.int32, (1, 1, wall), 2)
 
     def one_slot(s, carry):
-        @pl.when(ids[s] >= 0)
-        def _():
-            n = ids[s]
+        if True:
+            n = lax.max(ids[s], 0)
+            living = jnp.where(ids[s] >= 0, 1.0, 0.0)
             x0 = lax.rem(corners[0, s] - first_x + wide * nx, wide * nx)
             y0 = corners[1, s]
             z0 = lax.rem(corners[2, s] - first_z + tall * nz, tall * nz)
@@ -323,7 +330,7 @@
             for c in range(3):
                 a, b = (c + 1) % 3, (c + 2) % 3
                 target = moving[c, n] + (spin[a] * lever[b : b + 1] - spin[b] * lever[a : a + 1])
-                loads.append((target - sampled[c : c + 1]) * weight_z)
+                loads.append((living * (target - sampled[c : c + 1])) * weight_z)
             load = parts(jnp.concatenate(loads))
             value = pair(load, (cross[s, 0], cross[s, 1]), 1).reshape(3, BAND, BOX * BAND)
             inside = (lane >= y0) & (lane < y0 + BOX)
@@ -335,24 +342,29 @@
 
         return carry
 
-    lax.fori_loop(0, ids.shape[0], one_slot, 0)
-
-
-def spread_forces(nx, nz, extended, cross, slot_ids, corners, cells, fracs, moving, turning):
-    _, slots, markers = cells.shape
+    def four_slots(h, carry):
+        for k in range(4):
+            one_slot(4 * h + k, carry)
+        return carry
+
+    lax.fori_loop(0, ids.shape[0] // 4, four_slots, 0)
+
+
+def spread_forces(nx, nz, extended, cross, tap, slot_ids, corners, cells, fracs, moving, turning):
     scalar = pl.BlockSpec(memory_space=pltpu.SMEM)
     vector = pl.BlockSpec(memory_space=pltpu.VMEM)
+    scalars = [
+        pltpu.with_memory_space_constraint(each, pltpu.HBM)
+        for each in (slot_ids, corners, moving, turning)
+    ]
     return pl.pallas_call(
         functools.partial(marker_kernel, nx, nz),
         out_shape=jax.ShapeDtypeStruct(extended.shape, jnp.float32),
-        in_specs=[scalar] * 4 + [vector] * 4,
+        in_specs=[scalar] * 4 + [vector] * 5,
         out_specs=vector,
-        scratch_shapes=[
-            pltpu.VMEM((4, 3, slots, markers), jnp.float32),
-        ],
         compiler_params=pltpu.CompilerParams(vmem_limit_bytes=16 << 20),
         name="markers",
-    )(slot_ids, corners, moving, turning, cells, fracs, extended, cross)
+    )(*scalars, cells, fracs, tap, extended, cross)
 
 
 def exchanged(rows, lane_bits):
@@ -733,16 +745,17 @@
     nx, nz, flow_state, slot_ids, corners, marker_cells, marker_frac, particle_velocity,
     particle_spin,
 ):
-    extended, cross = predict(flow_state, marker_cells, marker_frac, nx, nz)
+    extended, cross, tap, cells, fracs = predict(flow_state, marker_cells, marker_frac, nx, nz)
     force = spread_forces(
         nx,
         nz,
         extended,
         cross,
+        tap,
         slot_ids,
         corners,
-        marker_cells,
-        marker_frac,
+        cells,
+        fracs,
         particle_velocity,
         particle_spin,
     )

time: 99.6 us -> 92.7 us (0.931); the launches traced: 98.3 us -> 92.6 us
  local copies, waits for them, and re-layouts: 5.96 us -> 0.01 us
    pallas_call x1, Pallas kernels: 1.64 us -> 10.5 us  [spread_forces(): pl.pallas_call(functools.partial(marker_kernel, nx, nz), out_shape=jax.Sh...]
    pallas_call x1, Pallas kernels: 57.4 us -> 48.6 us  [spectrum(): pl.pallas_call(functools.partial(spectrum_kernel, nx, nz), out_shape=(jax...]
    unnamed x20 -> x4, local copies, waits for them, and re-layouts: 5.96 us -> 0.01 us
where the time goes in v5:
time: 92.7 us; the launch traced here: 92.6 us
  Pallas kernels  91.9 us (99%)
    pallas_call x1, Pallas kernels, spectrum(): pl.pallas_call(functools.partial(spectrum_kernel, nx, nz), out_shape=(jax...  48.6 us
    pallas_call x1, Pallas kernels, predict(): pl.pallas_call(functools.partial(front_kernel, nx, nz), out_shape=(jax.Sh...  30.5 us
    pallas_call x1, Pallas kernels, spread_forces(): pl.pallas_call(functools.partial(marker_kernel, nx, nz), out_shape=jax.Sh...  10.5 us
    pallas_call x1, Pallas kernels, spectrum(): pl.pallas_call(functools.partial(finish_kernel, 1.0 / math.sqrt(length_x...  2.21 us

profile of v5, /device:TPU:1, one launch (start us, length us, event | category | flops | bytes accessed | tf_op | source)
XLA Modules:
  0.0 92.6 jit_solution(16963172827897041741)
XLA Ops:
  0.6 30.5 %front.1 = (f32[3,40,64,128]{3,2,1,0:T(8,128)S(1)}, bf16[8,2,768,512]{3,2,1,0:T(8,128)(2,1)S(1)}, f32[4,3,8,512]{3,2,1,0:T(8,128)S(1)}, s32[3,8,512]{2,1,0:T(8,128)S(1)}, f32[3,8,512]{2,1,0:T(8,128)S(1)}) custom-call(f32[4,16,32,128]{3,2,1,0:T(8,128)} %flow_in.1, s32[3,8,512]{2,1,0:T(8,128)} %cells_in.1, f32[3,8,512]{2,1,0:T(8,128)} %fracs_in.1), custom_call_target="tpu_custom_call" | custom-call | tf_op jit(solution)/shard_map/front/pallas_call | solution.py:251
  31.2 0.0 copy-start.1
  31.2 10.5 %markers.1.force = f32[3,40,64,128]{3,2,1,0:T(8,128)S(1)} custom-call(s32[8]{0:T(128)} %ids.1, s32[3,8]{1,0:T(4,128)} %corners.1, f32[3,1024]{1,0:T(4,128)} %moving.1, f32[3,1024]{1,0:T(4,128)} %turning.1, s32[3,8,512]{2,1,0:T(8,128)S(1)} %get-tuple-element.9.cells, f32[3,8,512]{2,1,0:T(8,128)S(1)} %get-tuple-element.10.fracs, ...), custom_call_target="tpu_custom_call" | custom-call | tf_op jit(solution)/shard_map/markers/pallas_call | solution.py:360
  41.7 0.0 copy-done.1
  41.7 0.0 copy-start
  41.7 48.6 %spectrum.1 = (f32[3,16,32,128]{3,2,1,0:T(8,128)S(1)}, f32[32,2,8,256]{3,2,1,0:T(8,128)S(1)}) custom-call(f32[3,40,64,128]{3,2,1,0:T(8,128)S(1)} %markers.1.force, f32[3,40,64,128]{3,2,1,0:T(8,128)S(1)} %get-tuple-element.12.field, bf16[2,512,256]{2,1,0:T(8,128)(2,1)S(1)} %copy-done.1), custom_call_target="tpu_custom_call" | custom-call | tf_op jit(solution)/shard_map/spectrum/pallas_call | solution.py:694
  90.3 0.0 copy-done
  90.4 2.2 %finish.1 = (f32[3,16,32,128]{3,2,1,0:T(8,128)}, f32[2,16,8,512]{3,2,1,0:T(8,128)}) custom-call(f32[3,16,32,128]{3,2,1,0:T(8,128)S(1)} %get-tuple-element.14.velocity_in, f32[32,2,8,256]{3,2,1,0:T(8,128)S(1)} %get-tuple-element.15.rows, bf16[2,4,512,256]{3,2,1,0:T(8,128)(2,1)S(1)} %copy-done), custom_call_target="tpu_custom_call" | custom-call | tf_op jit(solution)/shard_map/finish/pallas_call | solution.py:727
Async XLA Ops:
  31.2 10.5 %copy-start.1 = (bf16[2,512,256]{2,1,0:T(8,128)(2,1)S(1)}, bf16[2,512,256]{2,1,0:T(8,128)(2,1)}, u32[]{:S(2)}) copy-start(bf16[2,512,256]{2,1,0:T(8,128)(2,1)} %constant.4.clone.table_z) | copy-start | bytes 1572868
  41.7 48.6 %copy-start = (bf16[2,4,512,256]{3,2,1,0:T(8,128)(2,1)S(1)}, bf16[2,4,512,256]{3,2,1,0:T(8,128)(2,1)}, u32[]{:S(2)}) copy-start(bf16[2,4,512,256]{3,2,1,0:T(8,128)(2,1)} %constant.5.clone.table_x) | copy-start | bytes 6291460

commit v6 on v5

--- a/solution.py
+++ b/solution.py
@@ -181,18 +181,20 @@
         at, height = lines[piece]
         slot = min(piece, 2)
         if piece != 3:
+            count = min(at + height, HALF) - at
             copy = remote(
-                field.at[c, columns, pl.ds(SIDE + at, half)],
-                field.at[c, columns, pl.ds(SIDE + tall + at, half)],
+                field.at[c, columns, pl.ds(SIDE + at, count)],
+                field.at[c, columns, pl.ds(SIDE + tall + at, count)],
                 (r_send, r_recv), (0, c, side, slot), below,
             )
             copy.start()
             z_copies.append(copy)
         if piece != 2:
-            start = at + height - half
+            start = max(at, tall - HALF)
+            count = at + height - start
             copy = remote(
-                field.at[c, columns, pl.ds(SIDE + start, half)],
-                field.at[c, columns, pl.ds(SIDE + start - tall, half)],
+                field.at[c, columns, pl.ds(SIDE + start, count)],
+                field.at[c, columns, pl.ds(SIDE + start - tall, count)],
                 (r_send, r_recv), (1, c, side, slot), above,
             )
             copy.start()
@@ -218,18 +220,21 @@
             send(c, piece)
     for c in range(3):
         down = remote(
-            field.at[c, own, pl.ds(SIDE, SIDE)],
-            field.at[c, own, pl.ds(SIDE + tall, SIDE)],
+            field.at[c, own, pl.ds(SIDE, HALF)],
+            field.at[c, own, pl.ds(SIDE + tall, HALF)],
             (z_send, z_recv), (0, c), below,
         )
         up = remote(
-            field.at[c, own, pl.ds(tall, SIDE)],
-            field.at[c, own, pl.ds(0, SIDE)],
+            field.at[c, own, pl.ds(SIDE + tall - HALF, HALF)],
+            field.at[c, own, pl.ds(SIDE - HALF, HALF)],
             (z_send, z_recv), (1, c), above,
         )
         down.start()
         up.start()
         z_copies.extend((down, up))
+    blank = jnp.zeros(field.shape[:2] + (SIDE - HALF, wall), jnp.float32)
+    field[:, :, pl.ds(0, SIDE - HALF), :] = blank
+    field[:, :, pl.ds(SIDE + tall + HALF, SIDE - HALF), :] = blank
     for load in lists:
         load.wait()
     cross_weights(cells, fracs, tap, cross)
@@ -408,6 +413,9 @@
     lax.fori_loop(1, nx, greet_x, 0)
     lax.fori_loop(1, nz, greet_z, 0)
     wide, tall = velocity.shape[1], velocity.shape[2]
+    blank = jnp.zeros(z_got.shape[1:3] + (SIDE - HALF, z_got.shape[4]), jnp.float32)
+    z_got[0, :, :, pl.ds(HALF, SIDE - HALF), :] = blank
+    z_got[1, :, :, pl.ds(0, SIDE - HALF), :] = blank
     row_out[0] = force[2, :, SIDE, :]
     row_out[1] = force[2, :, SIDE + tall - 1, :]
     pl.semaphore_wait(barrier, nx + nz - 2)
@@ -419,13 +427,13 @@
     def fold_z(c, piece):
         columns = pieces[piece]
         down = remote(
-            force.at[c, columns, pl.ds(0, SIDE), :],
-            z_got.at[1, c, columns],
+            force.at[c, columns, pl.ds(SIDE - HALF, HALF), :],
+            z_got.at[1, c, columns, pl.ds(SIDE - HALF, HALF), :],
             (z_send, z_recv), (1, c, piece), below,
         )
         up = remote(
-            force.at[c, columns, pl.ds(SIDE + tall, SIDE), :],
-            z_got.at[0, c, columns],
+            force.at[c, columns, pl.ds(SIDE + tall, HALF), :],
+            z_got.at[0, c, columns, pl.ds(0, HALF), :],
             (z_send, z_recv), (0, c, piece), above,
         )
         down.start()
@@ -433,21 +441,24 @@
         return [down, up]
 
     rims, inner = {}, {}
-    for c in order:
-        rims[c] = fold_z(c, 0) + fold_z(c, 1)
-        if c == 2:
-            lines = [
-                remote(row_out.at[0], row_got.at[1], (e_send, e_recv), 0, below),
-                remote(row_out.at[1], row_got.at[0], (e_send, e_recv), 1, above),
-            ]
-            for copy in lines:
-                copy.start()
-    for c in order:
-        inner[c] = fold_z(c, 2)
+    rims[0] = fold_z(0, 0) + fold_z(0, 1)
+    lines = [
+        remote(row_out.at[0], row_got.at[1], (e_send, e_recv), 0, below),
+        remote(row_out.at[1], row_got.at[0], (e_send, e_recv), 1, above),
+    ]
     x_copies = {}
     for c in order:
         for copy in rims[c]:
             copy.wait_recv()
+        if c == 0:
+            rims[2] = fold_z(2, 0) + fold_z(2, 1)
+            for copy in lines:
+                copy.start()
+            inner[0] = fold_z(0, 2)
+        if c == 2:
+            rims[1] = fold_z(1, 0) + fold_z(1, 1)
+            inner[2] = fold_z(2, 2)
+            inner[1] = fold_z(1, 2)
         for part in range(2):
             inside = pl.ds(part * SIDE, SIDE)
             outside = pl.ds(SIDE + part * SIDE, SIDE)

time: 92.7 us -> 91.2 us (0.984)
  Pallas kernels: 91.9 us -> 90.4 us
    pallas_call x1, Pallas kernels: 48.6 us -> 47.2 us  [spectrum(): pl.pallas_call(functools.partial(spectrum_kernel, nx, nz), out_shape=(jax...]
where the time goes in v6:
time: 91.2 us; the launch traced here: 91.1 us
  Pallas kernels  90.4 us (99%)
    pallas_call x1, Pallas kernels, spectrum(): pl.pallas_call(functools.partial(spectrum_kernel, nx, nz), out_shape=(jax...  47.2 us
    pallas_call x1, Pallas kernels, predict(): pl.pallas_call(functools.partial(front_kernel, nx, nz), out_shape=(jax.Sh...  30.5 us
    pallas_call x1, Pallas kernels, spread_forces(): pl.pallas_call(functools.partial(marker_kernel, nx, nz), out_shape=jax.Sh...  10.5 us
    pallas_call x1, Pallas kernels, spectrum(): pl.pallas_call(functools.partial(finish_kernel, 1.0 / math.sqrt(length_x...  2.21 us

profile of v6, /device:TPU:1, one launch (start us, length us, event | category | flops | bytes accessed | tf_op | source)
XLA Modules:
  0.0 91.1 jit_solution(12372511423845488959)
XLA Ops:
  0.6 30.5 %front.1 = (f32[3,40,64,128]{3,2,1,0:T(8,128)S(1)}, bf16[8,2,768,512]{3,2,1,0:T(8,128)(2,1)S(1)}, f32[4,3,8,512]{3,2,1,0:T(8,128)S(1)}, s32[3,8,512]{2,1,0:T(8,128)S(1)}, f32[3,8,512]{2,1,0:T(8,128)S(1)}) custom-call(f32[4,16,32,128]{3,2,1,0:T(8,128)} %flow_in.1, s32[3,8,512]{2,1,0:T(8,128)} %cells_in.1, f32[3,8,512]{2,1,0:T(8,128)} %fracs_in.1), custom_call_target="tpu_custom_call" | custom-call | tf_op jit(solution)/shard_map/front/pallas_call | solution.py:256
  31.1 0.0 copy-start.1
  31.1 10.5 %markers.1.force = f32[3,40,64,128]{3,2,1,0:T(8,128)S(1)} custom-call(s32[8]{0:T(128)} %ids.1, s32[3,8]{1,0:T(4,128)} %corners.1, f32[3,1024]{1,0:T(4,128)} %moving.1, f32[3,1024]{1,0:T(4,128)} %turning.1, s32[3,8,512]{2,1,0:T(8,128)S(1)} %get-tuple-element.9.cells, f32[3,8,512]{2,1,0:T(8,128)S(1)} %get-tuple-element.10.fracs, ...), custom_call_target="tpu_custom_call" | custom-call | tf_op jit(solution)/shard_map/markers/pallas_call | solution.py:365
  41.6 0.0 copy-done.1
  41.7 0.0 copy-start
  41.7 47.2 %spectrum.1 = (f32[3,16,32,128]{3,2,1,0:T(8,128)S(1)}, f32[32,2,8,256]{3,2,1,0:T(8,128)S(1)}) custom-call(f32[3,40,64,128]{3,2,1,0:T(8,128)S(1)} %markers.1.force, f32[3,40,64,128]{3,2,1,0:T(8,128)S(1)} %get-tuple-element.12.field, bf16[2,512,256]{2,1,0:T(8,128)(2,1)S(1)} %copy-done.1), custom_call_target="tpu_custom_call" | custom-call | tf_op jit(solution)/shard_map/spectrum/pallas_call | solution.py:705
  88.8 0.0 copy-done
  88.8 2.2 %finish.1 = (f32[3,16,32,128]{3,2,1,0:T(8,128)}, f32[2,16,8,512]{3,2,1,0:T(8,128)}) custom-call(f32[3,16,32,128]{3,2,1,0:T(8,128)S(1)} %get-tuple-element.14.velocity_in, f32[32,2,8,256]{3,2,1,0:T(8,128)S(1)} %get-tuple-element.15.rows, bf16[2,4,512,256]{3,2,1,0:T(8,128)(2,1)S(1)} %copy-done), custom_call_target="tpu_custom_call" | custom-call | tf_op jit(solution)/shard_map/finish/pallas_call | solution.py:738
Async XLA Ops:
  31.1 10.5 %copy-start.1 = (bf16[2,512,256]{2,1,0:T(8,128)(2,1)S(1)}, bf16[2,512,256]{2,1,0:T(8,128)(2,1)}, u32[]{:S(2)}) copy-start(bf16[2,512,256]{2,1,0:T(8,128)(2,1)} %constant.4.clone.table_z) | copy-start | bytes 1572868
  41.7 47.2 %copy-start = (bf16[2,4,512,256]{3,2,1,0:T(8,128)(2,1)S(1)}, bf16[2,4,512,256]{3,2,1,0:T(8,128)(2,1)}, u32[]{:S(2)}) copy-start(bf16[2,4,512,256]{3,2,1,0:T(8,128)(2,1)} %constant.5.clone.table_x) | copy-start | bytes 6291460

commit v7 on v6

--- a/solution.py
+++ b/solution.py
@@ -447,6 +447,26 @@
         remote(row_out.at[1], row_got.at[0], (e_send, e_recv), 1, above),
     ]
     x_copies = {}
+
+    def fold_x(c, source, columns, piece, start, count):
+        lines_at = pl.ds(start, count)
+        for side in range(2):
+            copy = remote(
+                source(side, c, columns[side], start, count),
+                x_got.at[1 - side, c, :, lines_at, :],
+                (x_send, x_recv), (1 - side, c, piece), (left, right)[side],
+            )
+            copy.start()
+            x_copies.setdefault(c, []).append(copy)
+
+    def from_force(side, c, columns, start, count):
+        return force.at[c, columns, pl.ds(SIDE + start, count), :]
+
+    def from_sums(side, c, columns, start, count):
+        return x_out.at[side, c, :, pl.ds(start, count), :]
+
+    for c in order:
+        fold_x(c, from_force, pieces, 0, HALF, tall - 2 * HALF)
     for c in order:
         for copy in rims[c]:
             copy.wait_recv()
@@ -466,11 +486,8 @@
                 x_out[side, c, :, inside, :] = (
                     force[c, pieces[side], outside, :] + z_got[part, c, pieces[side]]
                 )
-        back = remote(x_out.at[0, c], x_got.at[1, c], (x_send, x_recv), (1, c), left)
-        ahead = remote(x_out.at[1, c], x_got.at[0, c], (x_send, x_recv), (0, c), right)
-        back.start()
-        ahead.start()
-        x_copies[c] = [back, ahead]
+        fold_x(c, from_sums, pieces, 1, 0, HALF)
+        fold_x(c, from_sums, pieces, 2, tall - HALF, HALF)
         if c == 2:
             for copy in lines:
                 copy.wait_recv()
@@ -511,6 +528,17 @@
                 field[c, own, outside, :] + force[c, own, outside, :] + z_got[part, c, own]
             )
     for c in order:
+        if c == 1:
+            stream, span = velocity[0], velocity[2]
+            divergence = jnp.concatenate([stream[1:], edge_u[1:2]], axis=0) - jnp.concatenate(
+                [edge_u[0:1], stream[:-1]], axis=0
+            )
+            row = lax.broadcasted_iota(jnp.int32, (1, tall, 1), 1)
+            after = jnp.where(
+                row == tall - 1, edge_w[1][:, None, :], pltpu.roll(span, tall - 1, 1)
+            )
+            before = jnp.where(row == 0, edge_w[0][:, None, :], pltpu.roll(span, 1, 1))
+            divergence += after - before
         for copy in x_copies[c]:
             copy.wait_recv()
         velocity[c, pl.ds(0, HALF)] += x_got[0, c]
@@ -534,16 +562,7 @@
     normal = velocity[1]
     upper = jnp.where(lane == wall - 1, 0.0, pltpu.roll(normal, wall - 1, 2))
     lower = jnp.where(lane == 0, 0.0, pltpu.roll(normal, 1, 2))
-    divergence = upper - lower
-    stream = velocity[0]
-    divergence += jnp.concatenate([stream[1:], edge_u[1:2]], axis=0) - jnp.concatenate(
-        [edge_u[0:1], stream[:-1]], axis=0
-    )
-    span = velocity[2]
-    row = lax.broadcasted_iota(jnp.int32, (1, tall, 1), 1)
-    after = jnp.where(row == tall - 1, edge_w[1][:, None, :], pltpu.roll(span, tall - 1, 1))
-    before = jnp.where(row == 0, edge_w[0][:, None, :], pltpu.roll(span, 1, 1))
-    divergence = (divergence + (after - before)) * 0.5
+    divergence = (divergence + (upper - lower)) * 0.5
     for half in range(wide // 8):
         blocks = exchanged([divergence[half * 8 + i] for i in range(8)], (16, 32, 64))
         for j in range(nz):
@@ -726,7 +745,7 @@
             pltpu.VMEM((nz, tall, wide * each), jnp.float32),
             pltpu.VMEM((nz, tall, wide * each), jnp.float32),
             pltpu.VMEM((2, nx, modes, wide * each), jnp.float32),
-            dma((2, 3, 3)), dma((2, 3, 3)), dma((2, 3)), dma((2, 3)), dma((6,)), dma((6,)),
+            dma((2, 3, 3)), dma((2, 3, 3)), dma((2, 3, 3)), dma((2, 3, 3)), dma((6,)), dma((6,)),
             dma((nz,)), dma((nz,)), dma((nx,)), dma((nx,)),
         ],
         compiler_params=pltpu.CompilerParams(

time: 91.2 us -> 89.6 us (0.982)
  Pallas kernels: 90.4 us -> 88.8 us
    pallas_call x1, Pallas kernels: 47.2 us -> 45.6 us  [spectrum(): pl.pallas_call(functools.partial(spectrum_kernel, nx, nz), out_shape=(jax...]
where the time goes in v7:
time: 89.6 us; the launch traced here: 89.5 us
  Pallas kernels  88.8 us (99%)
    pallas_call x1, Pallas kernels, spectrum(): pl.pallas_call(functools.partial(spectrum_kernel, nx, nz), out_shape=(jax...  45.6 us
    pallas_call x1, Pallas kernels, predict(): pl.pallas_call(functools.partial(front_kernel, nx, nz), out_shape=(jax.Sh...  30.5 us
    pallas_call x1, Pallas kernels, spread_forces(): pl.pallas_call(functools.partial(marker_kernel, nx, nz), out_shape=jax.Sh...  10.5 us
    pallas_call x1, Pallas kernels, spectrum(): pl.pallas_call(functools.partial(finish_kernel, 1.0 / math.sqrt(length_x...  2.22 us

profile of v7, /device:TPU:1, one launch (start us, length us, event | category | flops | bytes accessed | tf_op | source)
XLA Modules:
  0.0 89.5 jit_solution(11194576250239764135)
XLA Ops:
  0.6 30.5 %front.1 = (f32[3,40,64,128]{3,2,1,0:T(8,128)S(1)}, bf16[8,2,768,512]{3,2,1,0:T(8,128)(2,1)S(1)}, f32[4,3,8,512]{3,2,1,0:T(8,128)S(1)}, s32[3,8,512]{2,1,0:T(8,128)S(1)}, f32[3,8,512]{2,1,0:T(8,128)S(1)}) custom-call(f32[4,16,32,128]{3,2,1,0:T(8,128)} %flow_in.1, s32[3,8,512]{2,1,0:T(8,128)} %cells_in.1, f32[3,8,512]{2,1,0:T(8,128)} %fracs_in.1), custom_call_target="tpu_custom_call" | custom-call | tf_op jit(solution)/shard_map/front/pallas_call | solution.py:256
  31.1 0.0 copy-start.1
  31.1 10.5 %markers.1.force = f32[3,40,64,128]{3,2,1,0:T(8,128)S(1)} custom-call(s32[8]{0:T(128)} %ids.1, s32[3,8]{1,0:T(4,128)} %corners.1, f32[3,1024]{1,0:T(4,128)} %moving.1, f32[3,1024]{1,0:T(4,128)} %turning.1, s32[3,8,512]{2,1,0:T(8,128)S(1)} %get-tuple-element.9.cells, f32[3,8,512]{2,1,0:T(8,128)S(1)} %get-tuple-element.10.fracs, ...), custom_call_target="tpu_custom_call" | custom-call | tf_op jit(solution)/shard_map/markers/pallas_call | solution.py:365
  41.6 0.0 copy-done.1
  41.6 0.0 copy-start
  41.7 45.6 %spectrum.1 = (f32[3,16,32,128]{3,2,1,0:T(8,128)S(1)}, f32[32,2,8,256]{3,2,1,0:T(8,128)S(1)}) custom-call(f32[3,40,64,128]{3,2,1,0:T(8,128)S(1)} %markers.1.force, f32[3,40,64,128]{3,2,1,0:T(8,128)S(1)} %get-tuple-element.12.field, bf16[2,512,256]{2,1,0:T(8,128)(2,1)S(1)} %copy-done.1), custom_call_target="tpu_custom_call" | custom-call | tf_op jit(solution)/shard_map/spectrum/pallas_call | solution.py:724
  87.3 0.0 copy-done
  87.3 2.2 %finish.1 = (f32[3,16,32,128]{3,2,1,0:T(8,128)}, f32[2,16,8,512]{3,2,1,0:T(8,128)}) custom-call(f32[3,16,32,128]{3,2,1,0:T(8,128)S(1)} %get-tuple-element.14.velocity_in, f32[32,2,8,256]{3,2,1,0:T(8,128)S(1)} %get-tuple-element.15.rows, bf16[2,4,512,256]{3,2,1,0:T(8,128)(2,1)S(1)} %copy-done), custom_call_target="tpu_custom_call" | custom-call | tf_op jit(solution)/shard_map/finish/pallas_call | solution.py:757
Async XLA Ops:
  31.1 10.5 %copy-start.1 = (bf16[2,512,256]{2,1,0:T(8,128)(2,1)S(1)}, bf16[2,512,256]{2,1,0:T(8,128)(2,1)}, u32[]{:S(2)}) copy-start(bf16[2,512,256]{2,1,0:T(8,128)(2,1)} %constant.4.clone.table_z) | copy-start | bytes 1572868
  41.6 45.6 %copy-start = (bf16[2,4,512,256]{3,2,1,0:T(8,128)(2,1)S(1)}, bf16[2,4,512,256]{3,2,1,0:T(8,128)(2,1)}, u32[]{:S(2)}) copy-start(bf16[2,4,512,256]{3,2,1,0:T(8,128)(2,1)} %constant.5.clone.table_x) | copy-start | bytes 6291460

commit v8 on v7

--- a/solution.py
+++ b/solution.py
@@ -347,12 +347,12 @@
 
         return carry
 
-    def four_slots(h, carry):
-        for k in range(4):
-            one_slot(4 * h + k, carry)
+    def eight_slots(h, carry):
+        for k in range(8):
+            one_slot(8 * h + k, carry)
         return carry
 
-    lax.fori_loop(0, ids.shape[0] // 4, four_slots, 0)
+    lax.fori_loop(0, ids.shape[0] // 8, eight_slots, 0)
 
 
 def spread_forces(nx, nz, extended, cross, tap, slot_ids, corners, cells, fracs, moving, turning):

time: 89.6 us -> 89.1 us (level)
  no operation moved by 1% of the time
where the time goes in v8:
time: 89.1 us; the launch traced here: 88.9 us
  Pallas kernels  88.2 us (99%)
    pallas_call x1, Pallas kernels, spectrum(): pl.pallas_call(functools.partial(spectrum_kernel, nx, nz), out_shape=(jax...  45.5 us
    pallas_call x1, Pallas kernels, predict(): pl.pallas_call(functools.partial(front_kernel, nx, nz), out_shape=(jax.Sh...  30.5 us
    pallas_call x1, Pallas kernels, spread_forces(): pl.pallas_call(functools.partial(marker_kernel, nx, nz), out_shape=jax.Sh...  10 us
    pallas_call x1, Pallas kernels, spectrum(): pl.pallas_call(functools.partial(finish_kernel, 1.0 / math.sqrt(length_x...  2.21 us

profile of v8, /device:TPU:1, one launch (start us, length us, event | category | flops | bytes accessed | tf_op | source)
XLA Modules:
  0.0 88.9 jit_solution(7562547668926005332)
XLA Ops:
  0.6 30.5 %front.1 = (f32[3,40,64,128]{3,2,1,0:T(8,128)S(1)}, bf16[8,2,768,512]{3,2,1,0:T(8,128)(2,1)S(1)}, f32[4,3,8,512]{3,2,1,0:T(8,128)S(1)}, s32[3,8,512]{2,1,0:T(8,128)S(1)}, f32[3,8,512]{2,1,0:T(8,128)S(1)}) custom-call(f32[4,16,32,128]{3,2,1,0:T(8,128)} %flow_in.1, s32[3,8,512]{2,1,0:T(8,128)} %cells_in.1, f32[3,8,512]{2,1,0:T(8,128)} %fracs_in.1), custom_call_target="tpu_custom_call" | custom-call | tf_op jit(solution)/shard_map/front/pallas_call | solution.py:256
  31.1 0.0 copy-start.1
  31.1 10.0 %markers.1.force = f32[3,40,64,128]{3,2,1,0:T(8,128)S(1)} custom-call(s32[8]{0:T(128)} %ids.1, s32[3,8]{1,0:T(4,128)} %corners.1, f32[3,1024]{1,0:T(4,128)} %moving.1, f32[3,1024]{1,0:T(4,128)} %turning.1, s32[3,8,512]{2,1,0:T(8,128)S(1)} %get-tuple-element.9.cells, f32[3,8,512]{2,1,0:T(8,128)S(1)} %get-tuple-element.10.fracs, ...), custom_call_target="tpu_custom_call" | custom-call | tf_op jit(solution)/shard_map/markers/pallas_call | solution.py:365
  41.1 0.0 copy-done.1
  41.1 0.0 copy-start
  41.2 45.5 %spectrum.1 = (f32[3,16,32,128]{3,2,1,0:T(8,128)S(1)}, f32[32,2,8,256]{3,2,1,0:T(8,128)S(1)}) custom-call(f32[3,40,64,128]{3,2,1,0:T(8,128)S(1)} %markers.1.force, f32[3,40,64,128]{3,2,1,0:T(8,128)S(1)} %get-tuple-element.12.field, bf16[2,512,256]{2,1,0:T(8,128)(2,1)S(1)} %copy-done.1), custom_call_target="tpu_custom_call" | custom-call | tf_op jit(solution)/shard_map/spectrum/pallas_call | solution.py:724
  86.7 0.0 copy-done
  86.7 2.2 %finish.1 = (f32[3,16,32,128]{3,2,1,0:T(8,128)}, f32[2,16,8,512]{3,2,1,0:T(8,128)}) custom-call(f32[3,16,32,128]{3,2,1,0:T(8,128)S(1)} %get-tuple-element.14.velocity_in, f32[32,2,8,256]{3,2,1,0:T(8,128)S(1)} %get-tuple-element.15.rows, bf16[2,4,512,256]{3,2,1,0:T(8,128)(2,1)S(1)} %copy-done), custom_call_target="tpu_custom_call" | custom-call | tf_op jit(solution)/shard_map/finish/pallas_call | solution.py:757
Async XLA Ops:
  31.1 10.0 %copy-start.1 = (bf16[2,512,256]{2,1,0:T(8,128)(2,1)S(1)}, bf16[2,512,256]{2,1,0:T(8,128)(2,1)}, u32[]{:S(2)}) copy-start(bf16[2,512,256]{2,1,0:T(8,128)(2,1)} %constant.4.clone.table_z) | copy-start | bytes 1572868
  41.1 45.6 %copy-start = (bf16[2,4,512,256]{3,2,1,0:T(8,128)(2,1)S(1)}, bf16[2,4,512,256]{3,2,1,0:T(8,128)(2,1)}, u32[]{:S(2)}) copy-start(bf16[2,4,512,256]{3,2,1,0:T(8,128)(2,1)} %constant.5.clone.table_x) | copy-start | bytes 6291460
